TPU v7x, 32 devices: a whole 2x2x4 slice. The times are simulated.
32 devices in a mesh: seq: 16 (over z, y, core), head: 2 (over x).
Axes of the slice: x: 2, y: 2, z: 4, core: 2. Of those that a mesh axis runs over, the one named last changes fastest.
Arguments:
- tokens: bfloat16 [8192, 1024], P('seq'), may hold values from -24 to 24
- norm_attn: float32 [1024], replicated, may hold values from 0.5 to 1.5
- self_qkv: bfloat16 [3, 1024, 1024], P(None, None, 'head'), may hold values from -4 to 4
- self_out: bfloat16 [1024, 1024], P('head'), may hold values from -0.1875 to 0.1875
- norm_ffn: float32 [1024], replicated, may hold values from 0.5 to 1.5
- ffn_in: bfloat16 [2, 1024, 2816], P(None, None, 'head'), may hold values from -0.1875 to 0.1875
- ffn_out: bfloat16 [2816, 1024], P('head'), may hold values from -0.109375 to 0.109375
- norm_final: float32 [1024], replicated, may hold values from 0.5 to 1.5
- pad_lengths: int32 [16], replicated, may hold values from 64 to 512
- targets: bfloat16 [512, 1024], replicated, may hold values from -8 to 8
- target_lengths: int32 [4], replicated, may hold values from 32 to 128
- norm_cross: float32 [1024], replicated, may hold values from 0.1 to 1.9
- cross_query: bfloat16 [1024, 1024], P(None, 'head'), may hold values from -4 to 4
- cross_kv: bfloat16 [2, 1024, 1024], P(None, None, 'head'), may hold values from -4 to 4
- cross_out: bfloat16 [1024, 1024], P('head'), may hold values from -4 to 4
Outputs:
- encoded: bfloat16 [8192, 1024], P('seq')
- decoded: bfloat16 [512, 1024], replicated
All inputs are finite; a program needn't handle non-finite values.
Results may differ from a plain program's by a relative error of at most 0.033.
Values may be sent and summed in bfloat16 or wider, within the bound.
A program may use at most 128 MiB of HBM per device.

v0:
```python
import functools
import math

import jax
import jax.numpy as jnp
from jax import lax
from jax.experimental import pallas as pl
from jax.experimental.pallas import tpu as pltpu
from jax.sharding import PartitionSpec as P

HD = 64
TOK_DEV = 512
TGT_LEN = 128

epsilon = 1e-06
masked_score = -1e30
MESH = pl.DeviceIdType.MESH


def greet_all(ring, sides):
    me = lax.axis_index("seq")
    here = lax.axis_index("head")
    barrier = pltpu.get_barrier_semaphore()

    def greet(i, carry):
        pl.semaphore_signal(
            barrier, inc=1, device_id={"seq": lax.rem(me + i, ring)}, device_id_type=MESH
        )
        return carry

    lax.fori_loop(1, ring, greet, 0)
    for k in range(1, sides):
        pl.semaphore_signal(
            barrier, inc=1, device_id={"head": lax.rem(here + k, sides)}, device_id_type=MESH
        )
    pl.semaphore_wait(barrier, ring - 1 + sides - 1)


def side_copy(sides, k, source, target, send_sem, recv_sem):
    here = lax.axis_index("head")
    return pltpu.make_async_remote_copy(
        src_ref=source,
        dst_ref=target,
        send_sem=send_sem,
        recv_sem=recv_sem,
        device_id={"head": lax.rem(here + k, sides)},
        device_id_type=MESH,
    )


def scatter_kernel(
    ring, share, sides, q_in, kv_in, w_in, targets, g_cross, w_cross,
    q_out, kv_out, w_out, cross_q, qs, qr, ks, kr, fs, fr, ls, ws, wr,
):
    me = lax.axis_index("seq")
    here = lax.axis_index("head")
    part = kv_in.shape[1]
    mine = pl.ds(pl.multiple_of(lax.rem(me, share) * part, part), part)
    own_q = pltpu.make_async_copy(q_in.at[me], q_out.at[me], ls.at[0])
    own_kv = pltpu.make_async_copy(kv_in.at[me], kv_out.at[me, mine], ls.at[1])
    own_q.start()
    own_kv.start()
    own_w = pltpu.make_async_copy(w_in, w_out.at[here], ls.at[2])
    own_w.start()
    greet_all(ring, sides)

    def q_copy(i):
        to = lax.rem(me + i, ring)
        return pltpu.make_async_remote_copy(
            src_ref=q_in.at[to],
            dst_ref=q_out.at[me],
            send_sem=qs.at[i],
            recv_sem=qr.at[i],
            device_id={"seq": to},
            device_id_type=MESH,
        )

    def kv_copy(i):
        to = lax.rem(me + i, ring)
        rows = pl.ds(pl.multiple_of(lax.rem(to, share) * part, part), part)
        return pltpu.make_async_remote_copy(
            src_ref=kv_in.at[to],
            dst_ref=kv_out.at[me, rows],
            send_sem=ks.at[i],
            recv_sem=kr.at[i],
            device_id={"seq": to},
            device_id_type=MESH,
        )

    def forward(i, k):
        origin = lax.rem(me - i + ring, ring)
        slot = lax.rem(me, share)
        to = me - slot + lax.rem(slot + k, share)
        block = kv_out.at[origin, mine]
        return pltpu.make_async_remote_copy(
            src_ref=block,
            dst_ref=block,
            send_sem=fs.at[i, k],
            recv_sem=fr.at[i, k],
            device_id={"seq": to},
            device_id_type=MESH,
        )

    def arrived(i, k):
        slot = lax.rem(me, share)
        giver = me - slot + lax.rem(slot - k + share, share)
        origin = lax.rem(giver - i + ring, ring)
        rows = pl.ds(pl.multiple_of(lax.rem(giver, share) * part, part), part)
        block = kv_out.at[origin, rows]
        return pltpu.make_async_remote_copy(
            src_ref=block,
            dst_ref=block,
            send_sem=fs.at[i, k],
            recv_sem=fr.at[i, k],
            device_id={"seq": giver},
            device_id_type=MESH,
        )

    def send(i, carry):
        kv_copy(i).start()
        q_copy(i).start()
        return carry

    lax.fori_loop(1, ring, send, 0)
    for k in range(1, sides):
        side_copy(sides, k, w_in, w_out.at[here], ws.at[k], wr.at[k]).start()
    own_kv.wait()
    cross_normed = norm_rows(targets[...].astype(jnp.float32), g_cross[...]).astype(jnp.bfloat16)
    cross_q[...] = jnp.dot(
        cross_normed, w_cross[...], preferred_element_type=jnp.float32
    ).astype(jnp.bfloat16) * jnp.bfloat16(HD ** (-0.5))
    for k in range(1, share):
        forward(0, k).start()

    def relay(i, carry):
        pltpu.make_async_remote_copy(
            src_ref=kv_in.at[0],
            dst_ref=kv_out.at[lax.rem(me - i + ring, ring), mine],
            send_sem=ks.at[i],
            recv_sem=kr.at[i],
            device_id={"seq": lax.rem(me + i, ring)},
            device_id_type=MESH,
        ).wait_recv()
        for k in range(1, share):
            forward(i, k).start()
        return carry

    lax.fori_loop(1, ring, relay, 0)

    def finish(i, carry):
        pltpu.make_async_remote_copy(
            src_ref=q_in.at[0],
            dst_ref=q_out.at[lax.rem(me - i + ring, ring)],
            send_sem=qs.at[i],
            recv_sem=qr.at[i],
            device_id={"seq": lax.rem(me + i, ring)},
            device_id_type=MESH,
        ).wait_recv()
        q_copy(i).wait_send()
        kv_copy(i).wait_send()
        return carry

    lax.fori_loop(1, ring, finish, 0)

    def drain(i, carry):
        for k in range(1, share):
            arrived(i, k).wait_recv()
            forward(i, k).wait_send()
        return carry

    lax.fori_loop(0, ring, drain, 0)
    for k in range(1, sides):
        origin = lax.rem(here - k + sides, sides)
        side_copy(sides, k, w_in, w_out.at[origin], ws.at[k], wr.at[k]).wait()
    own_q.wait()
    own_w.wait()


def scatter_heads(ring, share, sides, q_send, kv_send, weights, targets, g_cross, w_cross):
    part = kv_send.shape[1]
    return pl.pallas_call(
        functools.partial(scatter_kernel, ring, share, sides),
        out_shape=(
            jax.ShapeDtypeStruct(q_send.shape, q_send.dtype),
            jax.ShapeDtypeStruct((ring, part * share, 2 * HD), kv_send.dtype),
            jax.ShapeDtypeStruct((sides,) + weights.shape, weights.dtype),
            jax.ShapeDtypeStruct((targets.shape[0], w_cross.shape[1]), jnp.bfloat16),
        ),
        in_specs=[pl.BlockSpec(memory_space=pltpu.VMEM)] * 6,
        out_specs=(pl.BlockSpec(memory_space=pltpu.VMEM),) * 4,
        scratch_shapes=[
            pltpu.SemaphoreType.DMA((ring,)),
            pltpu.SemaphoreType.DMA((ring,)),
            pltpu.SemaphoreType.DMA((ring,)),
            pltpu.SemaphoreType.DMA((ring,)),
            pltpu.SemaphoreType.DMA((ring, share)),
            pltpu.SemaphoreType.DMA((ring, share)),
            pltpu.SemaphoreType.DMA((3,)),
            pltpu.SemaphoreType.DMA((sides,)),
            pltpu.SemaphoreType.DMA((sides,)),
        ],
        compiler_params=pltpu.CompilerParams(
            collective_id=0, has_side_effects=True, vmem_limit_bytes=40 * 1024 * 1024
        ),
        name="scatter_heads",
    )(q_send, kv_send, weights, targets, g_cross[None, :], w_cross)


def norm_rows(values, gain):
    scale = lax.rsqrt(jnp.mean(values * values, axis=-1, keepdims=True) + epsilon)
    return values * scale * gain


def block_kernel(
    ring, share, sides, x_in, w_out, tokens, g_ffn, g_final, up_hbm, down_hbm,
    kv_hbm, cross_q, bias, w_cross, mine, live,
    encoded, decoded,
    context, hidden, normed, parts, up, down, w_kv, cross_k, cross_v,
    mixed, stats, ss, rs, fs, fr, ps, pr, ls, *tail
):
    me = lax.axis_index("seq")
    here = lax.axis_index("head")
    heads = ring // share
    rows, width = tokens.shape
    up_load = pltpu.make_async_copy(up_hbm, up, ls.at[0])
    down_load = pltpu.make_async_copy(down_hbm, down, ls.at[1])
    kv_load = pltpu.make_async_copy(kv_hbm, w_kv, ls.at[3])
    up_load.start()
    down_load.start()
    kv_load.start()

    def place(side, origin):
        return context.at[lax.rem(origin, share), side * heads + lax.div(origin, share)]

    own = pltpu.make_async_copy(x_in.at[me], place(here, me), ls.at[2])
    own.start()
    greet_all(ring, sides)

    def outgoing(i):
        to = lax.rem(me + i, ring)
        return pltpu.make_async_remote_copy(
            src_ref=x_in.at[to],
            dst_ref=place(here, me),
            send_sem=ss.at[i],
            recv_sem=rs.at[i],
            device_id={"seq": to},
            device_id_type=MESH,
        )

    def relay(i, k):
        block = place(here, lax.rem(me - i + ring, ring))
        return side_copy(sides, k, block, block, fs.at[i, k], fr.at[i, k])

    def send(i, carry):
        outgoing(i).start()
        return carry

    lax.fori_loop(1, ring, send, 0)
    own.wait()
    for k in range(1, sides):
        relay(0, k).start()

    def pass_on(i, carry):
        pltpu.make_async_remote_copy(
            src_ref=x_in.at[0],
            dst_ref=place(here, lax.rem(me - i + ring, ring)),
            send_sem=ss.at[i],
            recv_sem=rs.at[i],
            device_id={"seq": lax.rem(me + i, ring)},
            device_id_type=MESH,
        ).wait_recv()
        for k in range(1, sides):
            relay(i, k).start()
        return carry

    lax.fori_loop(1, ring, pass_on, 0)

    def sent(i, carry):
        outgoing(i).wait_send()
        return carry

    lax.fori_loop(1, ring, sent, 0)

    def drain(i, carry):
        for k in range(1, sides):
            relay(i, k).wait_send()
            origin = lax.rem(here - k + sides, sides)
            block = place(origin, lax.rem(me - i + ring, ring))
            side_copy(sides, k, block, block, fs.at[i, k], fr.at[i, k]).wait_recv()
        return carry

    lax.fori_loop(0, ring, drain, 0)
    part = rows // share

    def project(c, carry):
        at = pl.ds(pl.multiple_of(c * part, part), part)
        flat = context[c].reshape(sides * heads * HD, part)
        total = tokens[at, :].astype(jnp.float32) + lax.dot_general(
            flat, w_out[...], (((0,), (0,)), ((), ())), preferred_element_type=jnp.float32
        )
        hidden[at, :] = total
        normed[at, :] = norm_rows(total, g_ffn[...]).astype(jnp.bfloat16)
        return carry

    lax.fori_loop(0, share, project, 0)
    up_load.wait()
    down_load.wait()
    chunk = math.gcd(rows, 128)
    chunks = rows // chunk

    def span(c):
        return pl.ds(pl.multiple_of(c * chunk, chunk), chunk)

    def swap(c, k, side):
        return side_copy(
            sides, k, parts.at[side, span(c)], parts.at[side, span(c)], ps.at[c, k], pr.at[c, k]
        )

    def feed(c, carry):
        x = normed[span(c), :]
        gate = jnp.dot(x, up[0], preferred_element_type=jnp.float32)
        lift = jnp.dot(x, up[1], preferred_element_type=jnp.float32)
        active = (jax.nn.gelu(gate, approximate=True) * lift).astype(jnp.bfloat16)
        parts[here, span(c), :] = jnp.dot(
            active, down[...], preferred_element_type=jnp.float32
        ).astype(jnp.bfloat16)
        for k in range(1, sides):
            swap(c, k, here).start()
        return carry

    lax.fori_loop(0, chunks, feed, 0)
    kv_load.wait()

    def close(c, carry):
        for k in range(1, sides):
            swap(c, k, here).wait_send()
            swap(c, k, lax.rem(here - k + sides, sides)).wait_recv()
        total = hidden[span(c), :]
        for side in range(sides):
            total = total + parts[side, span(c), :].astype(jnp.float32)
        done = norm_rows(total, g_final[...]).astype(jnp.bfloat16)
        encoded[span(c), :] = done
        cross_k[span(c), :] = jnp.dot(
            done, w_kv[0], preferred_element_type=jnp.float32
        ).astype(jnp.bfloat16)
        cross_v[span(c), :] = jnp.dot(
            done, w_kv[1], preferred_element_type=jnp.float32
        ).astype(jnp.bfloat16)
        return carry

    lax.fori_loop(0, chunks, close, 0)
    targets = cross_q.shape[0]
    lane = lax.broadcasted_iota(jnp.int32, (rows, 2 * HD), 1)
    out_lane = lax.broadcasted_iota(jnp.int32, (targets, 2 * HD), 1)
    ones = jnp.ones((rows, 2 * HD), jnp.bfloat16)
    stats[...] = jnp.where(out_lane < HD, 0.0, 1.0)

    def cross_pair(i, carry):
        cut = pl.ds(pl.multiple_of(i * 2 * HD, 2 * HD), 2 * HD)
        q_here = cross_q[:, cut]
        k_here = cross_k[:, cut]
        v_here = cross_v[:, cut]
        pieces = []
        seen = stats[...]
        for h in range(2):
            own = lane < HD if h == 0 else lane >= HD
            keys = jnp.where(own, k_here, jnp.zeros_like(ones))
            values = jnp.where(own, v_here, ones)
            scores = bias[...] + lax.dot_general(
                q_here, keys, (((1,), (1,)), ((), ())), preferred_element_type=jnp.float32
            )
            top = jnp.max(scores, axis=1, keepdims=True)
            weights = jnp.exp(scores - top).astype(jnp.bfloat16)
            piece = jnp.dot(weights, values, preferred_element_type=jnp.float32)
            total = piece[:, 2 * HD - 1 :] if h == 0 else piece[:, :1]
            seen = jnp.where(
                out_lane == 2 * i + h, top, jnp.where(out_lane == HD + 2 * i + h, total, seen)
            )
            pieces.append(piece)
        stats[...] = seen
        mixed[:, cut] = jnp.where(out_lane < HD, pieces[0], pieces[1]).astype(jnp.bfloat16)
        return carry

    lax.fori_loop(0, heads // 2, cross_pair, 0)
    merge_tail(ring, sides, mixed, stats, w_cross, mine, live, decoded, *tail)


def encoder_block(
    ring, share, sides, back, w_out, tokens, g_ffn, g_final, ffn_in, ffn_out, w_kv, cross_q, bias,
    w_cross, mine, live,
):
    rows, width = tokens.shape
    chunks = rows // math.gcd(rows, 128)
    vmem = pl.BlockSpec(memory_space=pltpu.VMEM)
    hbm = pl.BlockSpec(memory_space=pl.ANY)
    return pl.pallas_call(
        functools.partial(block_kernel, ring, share, sides),
        out_shape=(
            jax.ShapeDtypeStruct((rows, width), jnp.bfloat16),
            jax.ShapeDtypeStruct((cross_q.shape[0], width), jnp.bfloat16),
        ),
        in_specs=[vmem] * 5 + [hbm] * 3 + [vmem] * 5,
        out_specs=(vmem, vmem),
        scratch_shapes=[
            pltpu.VMEM((share, sides * (ring // share), HD, rows // share), jnp.bfloat16),
            pltpu.VMEM((rows, width), jnp.float32),
            pltpu.VMEM((rows, width), jnp.bfloat16),
            pltpu.VMEM((sides, rows, width), jnp.bfloat16),
            pltpu.VMEM(ffn_in.shape, jnp.bfloat16),
            pltpu.VMEM(ffn_out.shape, jnp.bfloat16),
            pltpu.VMEM(w_kv.shape, jnp.bfloat16),
            pltpu.VMEM((rows, w_kv.shape[2]), jnp.bfloat16),
            pltpu.VMEM((rows, w_kv.shape[2]), jnp.bfloat16),
            pltpu.VMEM(cross_q.shape, jnp.bfloat16),
            pltpu.VMEM((cross_q.shape[0], 2 * HD), jnp.float32),
            pltpu.SemaphoreType.DMA((ring,)),
            pltpu.SemaphoreType.DMA((ring,)),
            pltpu.SemaphoreType.DMA((ring, sides)),
            pltpu.SemaphoreType.DMA((ring, sides)),
            pltpu.SemaphoreType.DMA((chunks, sides)),
            pltpu.SemaphoreType.DMA((chunks, sides)),
            pltpu.SemaphoreType.DMA((4,)),
            pltpu.VMEM((ring, mine.shape[0], cross_q.shape[1]), jnp.bfloat16),
            pltpu.VMEM((ring, mine.shape[0], 2 * HD), jnp.float32),
            pltpu.VMEM((sides, mine.shape[0], width), jnp.bfloat16),
            pltpu.SemaphoreType.DMA((ring,)),
            pltpu.SemaphoreType.DMA((ring,)),
            pltpu.SemaphoreType.DMA((ring,)),
            pltpu.SemaphoreType.DMA((ring,)),
            pltpu.SemaphoreType.DMA((sides,)),
            pltpu.SemaphoreType.DMA((sides,)),
            pltpu.SemaphoreType.DMA((ring,)),
            pltpu.SemaphoreType.DMA((ring,)),
            pltpu.SemaphoreType.DMA((ring,)),
            pltpu.SemaphoreType.DMA((ring,)),
            pltpu.SemaphoreType.DMA((2,)),
        ],
        compiler_params=pltpu.CompilerParams(
            collective_id=1, has_side_effects=True, vmem_limit_bytes=50 * 1024 * 1024
        ),
        name="encoder_block",
    )(
        back, w_out, tokens, g_ffn[None, :], g_final[None, :], ffn_in, ffn_out, w_kv, cross_q, bias,
        w_cross, mine, live,
    )


def merge_tail(
    ring, sides, mixed, stats, w_ref, mine, live, decoded,
    got, got_stats, parts, ms, mr, ts, tr, ps, pr, ds, dr, fs, fr, ls,
):
    me = lax.axis_index("seq")
    here = lax.axis_index("head")
    rows, width = mine.shape
    mate = me + 1 - 2 * lax.rem(me, 2)

    def slab(owner):
        return pl.ds(pl.multiple_of(owner * rows, rows), rows)

    own_mixed = pltpu.make_async_copy(mixed.at[slab(me)], got.at[me], ls.at[0])
    own_stats = pltpu.make_async_copy(stats.at[slab(me)], got_stats.at[me], ls.at[1])
    own_mixed.start()
    own_stats.start()

    def copies(i, origin):
        to = lax.rem(me + i, ring)
        return (
            pltpu.make_async_remote_copy(
                src_ref=mixed.at[slab(to)],
                dst_ref=got.at[origin],
                send_sem=ms.at[i],
                recv_sem=mr.at[i],
                device_id={"seq": to},
                device_id_type=MESH,
            ),
            pltpu.make_async_remote_copy(
                src_ref=stats.at[slab(to)],
                dst_ref=got_stats.at[origin],
                send_sem=ts.at[i],
                recv_sem=tr.at[i],
                device_id={"seq": to},
                device_id_type=MESH,
            ),
        )

    def send(i, carry):
        for copy in copies(i, me):
            copy.start()
        return carry

    lax.fori_loop(1, ring, send, 0)

    def collect(i, carry):
        for copy in copies(i, lax.rem(me - i + ring, ring)):
            copy.wait()
        return carry

    lax.fori_loop(1, ring, collect, 0)
    own_mixed.wait()
    own_stats.wait()
    heads = w_ref.shape[0] // HD
    seen = got_stats[...]
    best = jnp.max(seen, axis=0, keepdims=True)
    grow = jnp.exp(seen - best)
    sums = pltpu.roll(seen.reshape(ring * rows, 2 * HD), HD, 1).reshape(ring, rows, 2 * HD)
    weight_sum = jnp.sum(grow * sums, axis=0, keepdims=True)
    factor = (grow / weight_sum).reshape(ring * rows, 2 * HD)
    lane = lax.broadcasted_iota(jnp.int32, (2 * HD, heads * HD), 1)
    row = lax.broadcasted_iota(jnp.int32, (2 * HD, heads * HD), 0)
    spread = jnp.where((lane >= row * HD) & (lane < row * HD + HD), 1.0, 0.0)
    factor = jnp.where(
        lax.broadcasted_iota(jnp.int32, factor.shape, 1) < heads, factor, 0.0
    )
    wide = jnp.dot(
        factor, spread, precision=lax.Precision.HIGHEST, preferred_element_type=jnp.float32
    ).reshape(ring, rows, heads * HD)
    context = jnp.sum(got[...].astype(jnp.float32) * wide, axis=0).astype(jnp.bfloat16)
    parts[here] = jnp.dot(context, w_ref[...], preferred_element_type=jnp.float32).astype(
        jnp.bfloat16
    )

    def swap(k, side):
        return side_copy(sides, k, parts.at[side], parts.at[side], ps.at[k], pr.at[k])

    for k in range(1, sides):
        swap(k, here).start()
    for k in range(1, sides):
        swap(k, here).wait_send()
        swap(k, lax.rem(here - k + sides, sides)).wait_recv()
    total = parts[0].astype(jnp.float32)
    for side in range(1, sides):
        total = total + parts[side].astype(jnp.float32)
    decoded[slab(me), :] = (
        mine[...].astype(jnp.float32) + jnp.where(live[...] > 0.0, total, 0.0)
    ).astype(jnp.bfloat16)

    def spread_out(j, owner):
        block = decoded.at[slab(owner)]
        return pltpu.make_async_remote_copy(
            src_ref=block,
            dst_ref=block,
            send_sem=ds.at[j],
            recv_sem=dr.at[j],
            device_id={"seq": lax.rem(me + 2 * j, ring)},
            device_id_type=MESH,
        )

    def hand_over(j, owner):
        block = decoded.at[slab(owner)]
        return pltpu.make_async_remote_copy(
            src_ref=block,
            dst_ref=block,
            send_sem=fs.at[j],
            recv_sem=fr.at[j],
            device_id={"seq": mate},
            device_id_type=MESH,
        )

    def share_out(j, carry):
        spread_out(j, me).start()
        return carry

    lax.fori_loop(1, ring // 2, share_out, 0)
    hand_over(0, me).start()

    def pass_on(j, carry):
        owner = lax.rem(me - 2 * j + ring, ring)
        spread_out(j, owner).wait_recv()
        hand_over(j, owner).start()
        return carry

    lax.fori_loop(1, ring // 2, pass_on, 0)

    def finish(j, carry):
        spread_out(j, me).wait_send()
        return carry

    lax.fori_loop(1, ring // 2, finish, 0)

    def drain(j, carry):
        hand_over(j, lax.rem(me - 2 * j + ring, ring)).wait_send()
        hand_over(j, lax.rem(mate - 2 * j + ring, ring)).wait_recv()
        return carry

    lax.fori_loop(0, ring // 2, drain, 0)


def project_kernel(share, tokens, gain, w_ref, q_out, kv_out):
    rows = tokens.shape[0]
    part = rows // share
    heads = w_ref.shape[2] // HD
    normed = norm_rows(tokens[...].astype(jnp.float32), gain[...]).astype(jnp.bfloat16)
    scaling = jnp.bfloat16(HD ** (-0.5))
    queries = (
        lax.dot_general(
            w_ref[0], normed, (((0,), (1,)), ((), ())), preferred_element_type=jnp.float32
        ).astype(jnp.bfloat16)
        * scaling
    )
    keys = jnp.dot(normed, w_ref[1], preferred_element_type=jnp.float32).astype(jnp.bfloat16)
    values = jnp.dot(normed, w_ref[2], preferred_element_type=jnp.float32).astype(jnp.bfloat16)
    for h in range(heads):
        cut = slice(h * HD, (h + 1) * HD)
        both = jnp.concatenate([keys[:, cut], values[:, cut]], axis=1)
        for s in range(share):
            at = slice(s * part, (s + 1) * part)
            q_out[h * share + s] = queries[cut, at]
            kv_out[h * share + s] = both[at, :]


def project_heads(share, tokens, gain, weights):
    rows = tokens.shape[0]
    heads = weights.shape[2] // HD
    part = rows // share
    vmem = pl.BlockSpec(memory_space=pltpu.VMEM)
    return pl.pallas_call(
        functools.partial(project_kernel, share),
        out_shape=(
            jax.ShapeDtypeStruct((heads * share, HD, part), jnp.bfloat16),
            jax.ShapeDtypeStruct((heads * share, part, 2 * HD), jnp.bfloat16),
        ),
        in_specs=[vmem, vmem, vmem],
        out_specs=(vmem, vmem),
        compiler_params=pltpu.CompilerParams(vmem_limit_bytes=40 * 1024 * 1024),
        name="project_heads",
    )(tokens, gain[None, :], weights)


def attend_kernel(lengths, q_ref, kv_ref, o_ref, keys, values, flipped, count):
    blocks, span, lanes = kv_ref.shape
    tile = span
    queries = q_ref.shape[1]
    group = math.gcd(queries, 256)
    ones_rows = flipped.shape[1] - HD
    lane = lax.broadcasted_iota(jnp.int32, (span, lanes), 1)
    row = lax.broadcasted_iota(jnp.int32, (span, lanes), 0)

    @pl.when(pl.program_id(0) == 0)
    def pack():
        def place(j, start):
            block = kv_ref[j]
            dead = jnp.where(row < lengths[j], 0.0, masked_score).astype(jnp.bfloat16)
            at = pl.ds(pl.multiple_of(start, 16), span)
            keys[at, :] = jnp.where(lane < HD, block, dead)
            values[at, :] = jnp.where(lane < HD, jnp.ones_like(block), block)
            return start + ((lengths[j] + 15) // 16) * 16

        stop = lax.fori_loop(0, blocks, place, 0)
        at = pl.ds(pl.multiple_of(stop, 16), span)
        keys[at, :] = jnp.where(lane < HD, 0.0, masked_score).astype(jnp.bfloat16)
        values[at, :] = jnp.zeros((span, lanes), jnp.bfloat16)
        count[0] = (stop + tile - 1) // tile

        def flip(t, carry):
            at = pl.ds(pl.multiple_of(t * tile, tile), tile)
            flipped[t] = values[at, :].T[HD - ones_rows :, :]
            return carry

        lax.fori_loop(0, count[0], flip, 0)

    spare = lax.broadcasted_iota(jnp.int32, (HD, queries), 0)
    pick = jnp.where(spare == 0, 1.0, 0.0).astype(jnp.bfloat16)
    q_wide = jnp.concatenate([q_ref[...], pick], axis=0)
    cuts = [slice(g, g + group) for g in range(0, queries, group)]

    def step(t, state):
        at = pl.ds(pl.multiple_of(t * tile, tile), tile)
        keys_here = keys[at, :]
        values_here = flipped[t]
        all_scores = [
            jnp.dot(keys_here, q_wide[:, cut], preferred_element_type=jnp.float32) for cut in cuts
        ]
        updated = []
        for scores, (top, mixed) in zip(all_scores, state):
            new_top = jnp.maximum(top, jnp.max(scores, axis=0, keepdims=True))
            weights = jnp.exp(scores - new_top).astype(jnp.bfloat16)
            part = jnp.dot(values_here, weights, preferred_element_type=jnp.float32)
            updated.append((new_top, mixed * jnp.exp(top - new_top) + part))
        return tuple(updated)

    start = tuple(
        (
            jnp.full((1, group), masked_score, jnp.float32),
            jnp.zeros((ones_rows + HD, group), jnp.float32),
        )
        for cut in cuts
    )
    ends = lax.fori_loop(0, count[0], step, start)
    for cut, (top, mixed) in zip(cuts, ends):
        o_ref[:, cut] = (mixed[ones_rows:, :] / mixed[0:1, :]).astype(jnp.bfloat16)


def attend(q_all, kv_all, pad_lengths):
    blocks, span, lanes = kv_all.shape
    total = q_all.shape[1]
    width = math.gcd(total, 2048)
    return pl.pallas_call(
        attend_kernel,
        out_shape=jax.ShapeDtypeStruct((HD, total), jnp.bfloat16),
        grid_spec=pltpu.PrefetchScalarGridSpec(
            num_scalar_prefetch=1,
            grid=(total // width,),
            in_specs=[
                pl.BlockSpec((HD, width), lambda i, lengths: (0, i)),
                pl.BlockSpec((blocks, span, lanes), lambda i, lengths: (0, 0, 0)),
            ],
            out_specs=pl.BlockSpec((HD, width), lambda i, lengths: (0, i)),
            scratch_shapes=[
                pltpu.VMEM(((blocks + 1) * span, lanes), jnp.bfloat16),
                pltpu.VMEM(((blocks + 1) * span, lanes), jnp.bfloat16),
                pltpu.VMEM((blocks + 1, HD + 16, span), jnp.bfloat16),
                pltpu.SMEM((1,), jnp.int32),
            ],
        ),
        compiler_params=pltpu.CompilerParams(
            dimension_semantics=("arbitrary",), vmem_limit_bytes=48 * 1024 * 1024
        ),
        name="attend",
    )(pad_lengths, q_all, kv_all)


def local(
    ring,
    sides,
    tokens,
    norm_attn,
    self_qkv,
    self_out,
    norm_ffn,
    ffn_in,
    ffn_out,
    norm_final,
    pad_lengths,
    targets,
    target_lengths,
    norm_cross,
    cross_query,
    cross_kv,
    cross_out,
):
    row_count = tokens.shape[0]
    heads_here = self_qkv.shape[2] // HD
    share = ring // heads_here
    part = row_count // share
    q_send, kv_send = project_heads(share, tokens, norm_attn, self_qkv)
    q_got, kv_got, out_all, cross_q = scatter_heads(
        ring, share, sides, q_send, kv_send, self_out, targets, norm_cross, cross_query
    )
    q_all = q_got.transpose(1, 0, 2).reshape(HD, ring * part)
    mixed_t = attend(q_all, kv_got, pad_lengths)
    back = mixed_t.reshape(HD, ring, part).transpose(1, 0, 2)
    my_length = lax.dynamic_slice_in_dim(pad_lengths, lax.axis_index("seq"), 1, 0)
    bias = jnp.where(
        jnp.arange(row_count, dtype=jnp.int32)[None, :] < my_length[0], 0.0, masked_score
    ).astype(jnp.float32)
    target_rows = targets.shape[0]
    slice_rows = target_rows // ring
    slots = lax.axis_index("seq") * slice_rows + jnp.arange(slice_rows, dtype=jnp.int32)
    owner = slots // TGT_LEN
    limits = jnp.sum(
        jnp.where(
            owner[:, None] == jnp.arange(target_lengths.shape[0])[None, :],
            target_lengths[None, :],
            0,
        ),
        axis=1,
    )
    target_live = slots % TGT_LEN < limits
    mine = lax.dynamic_slice_in_dim(targets, lax.axis_index("seq") * slice_rows, slice_rows, 0)
    live = jnp.broadcast_to(target_live[:, None], mine.shape).astype(jnp.float32)
    encoded, decoded = encoder_block(
        ring,
        share,
        sides,
        back,
        out_all.reshape(-1, out_all.shape[2]),
        tokens,
        norm_ffn,
        norm_final,
        ffn_in,
        ffn_out,
        cross_kv,
        cross_q,
        bias,
        cross_out,
        mine,
        live,
    )
    return (encoded, decoded)


def solution(mesh):
    ring = mesh.shape["seq"]
    sides = mesh.shape["head"]
    placed = (
        P("seq", None),
        P(),
        P(None, None, "head"),
        P("head", None),
        P(),
        P(None, None, "head"),
        P("head", None),
        P(),
        P(),
        P(),
        P(),
        P(),
        P(None, "head"),
        P(None, None, "head"),
        P("head", None),
    )
    return jax.shard_map(
        functools.partial(local, ring, sides),
        mesh=mesh,
        in_specs=placed,
        out_specs=(P("seq", None), P()),
        check_vma=False,
    )
```

profile of v0, /device:TPU:0, one launch (start us, length us, event | category | flops | bytes accessed | tf_op | source)
XLA Modules:
  0.0 181.0 jit_solution(7885590651572472929)
XLA Ops:
  0.6 0.0 copy-start
  0.6 1.2 copy-done
  1.9 0.0 copy-start.1
  1.9 1.9 %copy-done.1 = bf16[3,1024,512]{2,1,0:T(8,128)(2,1)S(1)} copy-done((bf16[3,1024,512]{2,1,0:T(8,128)(2,1)S(1)}, bf16[3,1024,512]{2,1,0:T(8,128)(2,1)}, u32[]{:S(2)}) %copy-start.1) | copy-done | bytes 3145752
  3.8 0.0 copy-start.6
  3.8 0.7 copy-done.6
  4.4 0.0 copy-start.3
  4.4 0.0 copy-start.4
  4.4 0.0 copy-start.5
  4.4 0.0 copy-start.7
  4.4 2.2 %project_heads.1 = (bf16[16,64,256]{2,1,0:T(8,128)(2,1)S(1)}, bf16[16,256,128]{2,1,0:T(8,128)(2,1)S(1)}) custom-call(bf16[512,1024]{1,0:T(8,128)(2,1)S(1)} %copy-done, f32[1,1024]{1,0:T(1,128)S(1)} %bitcast.21, bf16[3,1024,512]{2,1,0:T(8,128)(2,1)S(1)} %copy-done.1), custom_call_target="tpu_custom_call" | custom-call | tf_op jit(solution)/shard_map/project_heads/pallas_call | solution.py:616
  6.6 0.0 copy-done.3
  6.6 0.0 copy-done.4
  6.6 0.0 copy-done.5
  6.7 0.0 copy-done.7
  6.7 0.0 copy-start.10
  6.7 33.5 %scatter_heads.1 = (bf16[16,64,256]{2,1,0:T(8,128)(2,1)S(1)}, bf16[16,512,128]{2,1,0:T(8,128)(2,1)S(1)}, bf16[2,512,1024]{2,1,0:T(8,128)(2,1)S(1)}, bf16[512,512]{1,0:T(8,128)(2,1)S(1)}) custom-call(bf16[16,64,256]{2,1,0:T(8,128)(2,1)S(1)} %get-tuple-element.8.q_in, bf16[16,256,128]{2,1,0:T(8,128)(2,1)S(1)} %get-tuple-element.9.kv_in, ...), custom_call_target="tpu_custom_call" | custom-call | tf_op jit(solution)/shard_map/scatter_heads/pallas_call | solution.py:181
  40.2 0.0 copy-start.2
  40.2 1.3 copy-done.2
  41.5 0.0 copy-start.11
  41.5 0.0 copy-done.10
  41.5 34.3 %attend.1 = bf16[64,4096]{1,0:T(8,128)(2,1)S(1)} custom-call(s32[16]{0:T(128)S(1)} %copy-done.10, bf16[64,4096]{1,0:T(8,128)(2,1)S(1)} %bitcast.17, bf16[16,512,128]{2,1,0:T(8,128)(2,1)S(1)} %get-tuple-element.11.kv_ref), custom_call_target="tpu_custom_call" | custom-call | tf_op jit(solution)/shard_map/attend/pallas_call | solution.py:697
  75.9 0.6 dynamic_slice.6
  76.5 0.6 compare_select_fusion.bias
  77.2 0.0 copy-done.11
  77.2 0.1 select_reduce_fusion
  77.3 0.1 broadcast_in_dim.50.live
  77.4 0.0 copy-done.8
  77.4 0.0 copy-done.9
  77.4 101.7 %encoder_block.1 = (bf16[512,1024]{1,0:T(8,128)(2,1)S(1)}, bf16[512,1024]{1,0:T(8,128)(2,1)S(1)}) custom-call(bf16[16,64,256]{2,1,0:T(8,128)(2,1)S(1)} %bitcast.16, bf16[1024,1024]{1,0:T(8,128)(2,1)} %bitcast.19, bf16[512,1024]{1,0:T(8,128)(2,1)} %tokens.3, f32[1,1024]{1,0:T(1,128)S(1)} %bitcast.23, f32[1,1024]{1,0:T(1,128)S(1)} %bitcast.24, ...), custom_call_target="tpu_custom_call" | custom-call | tf_op jit(solution)/shard_map/encoder_block/pallas_call | solution.py:396
  179.0 1.0 copy.28
  180.0 1.0 copy.29
  (7 shorter events, 0.1 us)
Async XLA Ops:
  0.6 1.2 copy-start
  1.9 1.9 %copy-start.1 = (bf16[3,1024,512]{2,1,0:T(8,128)(2,1)S(1)}, bf16[3,1024,512]{2,1,0:T(8,128)(2,1)}, u32[]{:S(2)}) copy-start(bf16[3,1024,512]{2,1,0:T(8,128)(2,1)} %w_ref.1) | copy-start | bytes 9437188
  3.8 0.7 copy-start.6
  4.4 2.2 %copy-start.3 = (bf16[512,1024]{1,0:T(8,128)(2,1)S(1)}, bf16[512,1024]{1,0:T(8,128)(2,1)}, u32[]{:S(2)}) copy-start(bf16[512,1024]{1,0:T(8,128)(2,1)} %targets.1) | copy-start | bytes 3145732
  4.4 2.2 %copy-start.4 = (bf16[512,1024]{1,0:T(8,128)(2,1)S(1)}, bf16[512,1024]{1,0:T(8,128)(2,1)}, u32[]{:S(2)}) copy-start(bf16[512,1024]{1,0:T(8,128)(2,1)} %w_in.1) | copy-start | bytes 3145732
  4.4 2.2 %copy-start.5 = (bf16[1024,512]{1,0:T(8,128)(2,1)S(1)}, bf16[1024,512]{1,0:T(8,128)(2,1)}, u32[]{:S(2)}) copy-start(bf16[1024,512]{1,0:T(8,128)(2,1)} %w_cross.2) | copy-start | bytes 3145732
  4.4 2.2 %copy-start.7 = (f32[1024]{0:T(1024)S(1)}, f32[1024]{0:T(1024)}, u32[]{:S(2)}) copy-start(f32[1024]{0:T(1024)} %param.26) | copy-start | bytes 12292
  6.7 34.9 %copy-start.10 = (s32[16]{0:T(128)S(1)}, s32[16]{0:T(128)}, u32[]{:S(2)}) copy-start(s32[16]{0:T(128)} %lengths.1) | copy-start | bytes 196
  40.2 1.3 copy-start.2
  41.5 35.7 %copy-start.11 = (s32[4]{0:T(128)S(1)}, s32[4]{0:T(128)}, u32[]{:S(2)}) copy-start(s32[4]{0:T(128)} %param.25) | copy-start | bytes 52
  41.5 35.9 %copy-start.8 = (f32[1024]{0:T(1024)S(1)}, f32[1024]{0:T(1024)}, u32[]{:S(2)}) copy-start(f32[1024]{0:T(1024)} %param.19) | copy-start | bytes 12292
  41.5 35.9 %copy-start.9 = (f32[1024]{0:T(1024)S(1)}, f32[1024]{0:T(1024)}, u32[]{:S(2)}) copy-start(f32[1024]{0:T(1024)} %param.22) | copy-start | bytes 12292
where the time goes:
time: 182 us; the launch traced here: 181 us
  Pallas kernels  172 us (95%)
  local copies, waits for them, and re-layouts  7.85 us (4%)
    pallas_call x1, Pallas kernels, encoder_block(): pl.pallas_call(functools.partial(block_kernel, ring, share, sides), out_s...  102 us
    pallas_call x1, Pallas kernels, attend(): pl.pallas_call(attend_kernel, out_shape=jax.ShapeDtypeStruct((HD, total),...  34.3 us
    pallas_call x1, Pallas kernels, scatter_heads(): pl.pallas_call(functools.partial(scatter_kernel, ring, share, sides), out...  33.5 us
    unnamed x26, local copies, waits for them, and re-layouts  7.09 us

commit v1 on v0

v1 whole, which is shorter than its diff:
```python
import functools
import math

import jax
import jax.numpy as jnp
from jax import lax
from jax.experimental import pallas as pl
from jax.experimental.pallas import tpu as pltpu
from jax.sharding import PartitionSpec as P

HD = 64
TGT_LEN = 128

epsilon = 1e-06
masked_score = -1e30
MESH = pl.DeviceIdType.MESH


def flip(index, other, count):
    result = 0
    weight = 1
    while weight < count:
        digit = other // weight if isinstance(other, int) else lax.div(other, weight)
        result = result + lax.rem(lax.div(index, weight) + digit, 2) * weight
        weight *= 2
    return result


def rows_at(start, size, align):
    return pl.ds(pl.multiple_of(start, align), size)


def greet_all(ring, sides):
    me = lax.axis_index("seq")
    here = lax.axis_index("head")
    barrier = pltpu.get_barrier_semaphore()

    def greet(i, carry):
        pl.semaphore_signal(
            barrier, inc=1, device_id={"seq": lax.rem(me + i, ring)}, device_id_type=MESH
        )
        return carry

    lax.fori_loop(1, ring, greet, 0)
    for k in range(1, sides):
        pl.semaphore_signal(
            barrier, inc=1, device_id={"head": lax.rem(here + k, sides)}, device_id_type=MESH
        )
    pl.semaphore_wait(barrier, ring - 1 + sides - 1)


def seq_copy(to, source, target, send_sem, recv_sem):
    return pltpu.make_async_remote_copy(
        src_ref=source,
        dst_ref=target,
        send_sem=send_sem,
        recv_sem=recv_sem,
        device_id={"seq": to},
        device_id_type=MESH,
    )


def side_copy(sides, k, source, target, send_sem, recv_sem):
    here = lax.axis_index("head")
    return pltpu.make_async_remote_copy(
        src_ref=source,
        dst_ref=target,
        send_sem=send_sem,
        recv_sem=recv_sem,
        device_id={"head": lax.rem(here + k, sides)},
        device_id_type=MESH,
    )


def norm_rows(values, gain):
    scale = lax.rsqrt(jnp.mean(values * values, axis=-1, keepdims=True) + epsilon)
    return values * scale * gain


def scatter_kernel(
    ring, share, sides, tokens_hbm, gain_hbm, qkv_hbm, out_hbm, targets_hbm, g_cross_hbm, w_cross_hbm,
    q_out, kv_out, out_all, cross_q,
    tokens, gain, qkv, targets, g_cross, w_cross, normed, q_in, kv_in,
    qs, qr, ks, kr, fs, fr, ls, os, ws, wr,
):
    me = lax.axis_index("seq")
    here = lax.axis_index("head")
    half = targets.shape[0]
    part = kv_in.shape[1]
    heads = ring // share
    slot = lax.rem(me, share)
    mine = rows_at(slot * part, part, part)
    loads = [
        pltpu.make_async_copy(source, target, ls.at[n])
        for n, (source, target) in enumerate(
            [
                (tokens_hbm, tokens),
                (gain_hbm, gain),
                (qkv_hbm.at[1], qkv.at[1]),
                (qkv_hbm.at[2], qkv.at[2]),
                (qkv_hbm.at[0], qkv.at[0]),
                (targets_hbm.at[rows_at(lax.rem(me, 2) * half, half, half)], targets),
                (g_cross_hbm, g_cross),
                (w_cross_hbm, w_cross),
            ]
        )
    ]
    for load in loads:
        load.start()
    greet_all(ring, sides)
    for k in range(1, sides):
        side_copy(sides, k, out_hbm, out_all.at[here], ws.at[k], wr.at[k]).start()

    def q_copy(i):
        to = flip(me, i, ring)
        return seq_copy(to, q_in.at[to], q_out.at[me], qs.at[i], qr.at[i])

    def kv_copy(i):
        to = flip(me, i, ring)
        rows = rows_at(lax.rem(to, share) * part, part, part)
        return seq_copy(to, kv_in.at[to], kv_out.at[me, rows], ks.at[i], kr.at[i])

    def forward(i, k):
        block = kv_out.at[flip(me, i, ring), mine]
        to = me - slot + lax.rem(slot + k, share)
        return seq_copy(to, block, block, fs.at[i, k], fr.at[i, k])

    def arrived(i, k):
        giver = me - slot + lax.rem(slot - k + share, share)
        rows = rows_at(lax.rem(giver, share) * part, part, part)
        block = kv_out.at[flip(giver, i, ring), rows]
        return seq_copy(giver, block, block, fs.at[i, k], fr.at[i, k])

    loads[0].wait()
    loads[1].wait()
    normed[...] = norm_rows(tokens[...].astype(jnp.float32), gain[...]).astype(jnp.bfloat16)
    loads[2].wait()
    loads[3].wait()
    keys = jnp.dot(normed[...], qkv[1], preferred_element_type=jnp.float32).astype(jnp.bfloat16)
    values = jnp.dot(normed[...], qkv[2], preferred_element_type=jnp.float32).astype(jnp.bfloat16)
    for h in range(heads):
        cut = slice(h * HD, (h + 1) * HD)
        both = jnp.concatenate([keys[:, cut], values[:, cut]], axis=1)
        for s in range(share):
            kv_in[h * share + s] = both[s * part : (s + 1) * part, :]

    def send_kv(i, carry):
        kv_copy(ring - i).start()
        return carry

    lax.fori_loop(1, ring, send_kv, 0)
    own_kv = pltpu.make_async_copy(kv_in.at[me], kv_out.at[me, mine], os.at[1])
    own_kv.start()
    loads[4].wait()
    queries = lax.dot_general(
        qkv[0], normed[...], (((0,), (1,)), ((), ())), preferred_element_type=jnp.float32
    ).astype(jnp.bfloat16) * jnp.bfloat16(HD ** (-0.5))
    for h in range(heads):
        for s in range(share):
            q_in[h * share + s] = queries[h * HD : (h + 1) * HD, s * part : (s + 1) * part]

    def send_q(i, carry):
        q_copy(ring - i).start()
        return carry

    lax.fori_loop(1, ring, send_q, 0)
    own_q = pltpu.make_async_copy(q_in.at[me], q_out.at[me], os.at[0])
    own_q.start()
    own_kv.wait()
    for k in range(1, share):
        forward(0, k).start()
    for load in loads[5:]:
        load.wait()
    cross_normed = norm_rows(targets[...].astype(jnp.float32), g_cross[...]).astype(jnp.bfloat16)
    cross_q[...] = jnp.dot(
        cross_normed, w_cross[...], preferred_element_type=jnp.float32
    ).astype(jnp.bfloat16) * jnp.bfloat16(HD ** (-0.5))

    def relay(i, carry):
        origin = flip(me, i, ring)
        seq_copy(origin, kv_in.at[0], kv_out.at[origin, mine], ks.at[i], kr.at[i]).wait_recv()
        for k in range(1, share):
            forward(i, k).start()
        return carry

    lax.fori_loop(1, ring, relay, 0)

    def finish(i, carry):
        origin = flip(me, i, ring)
        seq_copy(origin, q_in.at[0], q_out.at[origin], qs.at[i], qr.at[i]).wait_recv()
        q_copy(i).wait_send()
        kv_copy(i).wait_send()
        return carry

    lax.fori_loop(1, ring, finish, 0)

    def drain(i, carry):
        for k in range(1, share):
            arrived(i, k).wait_recv()
            forward(i, k).wait_send()
        return carry

    lax.fori_loop(0, ring, drain, 0)
    for k in range(1, sides):
        origin = lax.rem(here - k + sides, sides)
        side_copy(sides, k, out_hbm, out_all.at[origin], ws.at[k], wr.at[k]).wait()
    own_q.wait()


def scatter_heads(ring, share, sides, tokens, gain, qkv, w_out, targets, g_cross, w_cross):
    rows, width = tokens.shape
    heads = ring // share
    part = rows // share
    half = targets.shape[0] // 2
    bf16 = jnp.bfloat16
    vmem = pl.BlockSpec(memory_space=pltpu.VMEM)
    hbm = pl.BlockSpec(memory_space=pltpu.HBM)
    dma = pltpu.SemaphoreType.DMA
    return pl.pallas_call(
        functools.partial(scatter_kernel, ring, share, sides),
        out_shape=(
            jax.ShapeDtypeStruct((ring, HD, part), bf16),
            jax.ShapeDtypeStruct((ring, rows, 2 * HD), bf16),
            jax.ShapeDtypeStruct((sides,) + w_out.shape, bf16),
            jax.ShapeDtypeStruct((half, w_cross.shape[1]), bf16),
        ),
        in_specs=[hbm] * 7,
        out_specs=(vmem, vmem, hbm, vmem),
        scratch_shapes=[
            pltpu.VMEM((rows, width), bf16),
            pltpu.VMEM((1, width), jnp.float32),
            pltpu.VMEM(qkv.shape, bf16),
            pltpu.VMEM((half, width), bf16),
            pltpu.VMEM((1, width), jnp.float32),
            pltpu.VMEM(w_cross.shape, bf16),
            pltpu.VMEM((rows, width), bf16),
            pltpu.VMEM((heads * share, HD, part), bf16),
            pltpu.VMEM((heads * share, part, 2 * HD), bf16),
            dma((ring,)),
            dma((ring,)),
            dma((ring,)),
            dma((ring,)),
            dma((ring, share)),
            dma((ring, share)),
            dma((8,)),
            dma((2,)),
            dma((sides,)),
            dma((sides,)),
        ],
        compiler_params=pltpu.CompilerParams(
            collective_id=0, has_side_effects=True, vmem_limit_bytes=40 * 1024 * 1024
        ),
        name="scatter_heads",
    )(tokens, gain[None, :], qkv, w_out, targets, g_cross[None, :], w_cross)


def block_kernel(
    ring, share, sides, x_in, pad_lengths, target_lengths, tokens_hbm, g_ffn_hbm, g_final_hbm,
    w_own_hbm, w_all_hbm, up_hbm, down_hbm, kv_hbm, cross_q, w_cross_hbm, targets_hbm,
    encoded, decoded,
    tokens, g_ffn, g_final, w_out, context, hidden, normed, parts, up, down, w_kv, w_cross, mine,
    cross_k, cross_v, mixed, stats, got, partial, incoming,
    ls, ss, rs, fs, fr, ps, pr, cs, cr, ms, mr, xs, xr, zs, zr, ys, yr, ws, wr, hs, hr,
):
    me = lax.axis_index("seq")
    here = lax.axis_index("head")
    heads = ring // share
    rows, width = tokens.shape
    slab = mine.shape[0]
    core = lax.rem(me, 2)
    mate = flip(me, 1, ring)

    def slab_start(owner):
        return (lax.rem(owner, 2) * (ring // 2) + lax.div(owner, 2)) * slab

    loads = [
        pltpu.make_async_copy(source, target, ls.at[n])
        for n, (source, target) in enumerate(
            [
                (tokens_hbm, tokens),
                (g_ffn_hbm, g_ffn),
                (w_own_hbm, w_out.at[here]),
                (up_hbm, up),
                (down_hbm, down),
                (g_final_hbm, g_final),
                (kv_hbm, w_kv),
                (w_cross_hbm, w_cross),
                (targets_hbm.at[rows_at(slab_start(me), slab, slab)], mine),
            ]
            + [
                (w_all_hbm.at[lax.rem(here + k, sides)], w_out.at[lax.rem(here + k, sides)])
                for k in range(1, sides)
            ]
        )
    ]
    for load in loads:
        load.start()

    def place(side, origin):
        return context.at[lax.rem(origin, share), side * heads + lax.div(origin, share)]

    own = pltpu.make_async_copy(x_in.at[me], place(here, me), ls.at[len(loads)])
    own.start()
    greet_all(ring, sides)

    def outgoing(i):
        to = flip(me, i, ring)
        return seq_copy(to, x_in.at[to], place(here, me), ss.at[i], rs.at[i])

    def relay(i, k):
        block = place(here, flip(me, i, ring))
        return side_copy(sides, k, block, block, fs.at[i, k], fr.at[i, k])

    def send(i, carry):
        outgoing(ring - i).start()
        return carry

    lax.fori_loop(1, ring, send, 0)
    own.wait()
    for k in range(1, sides):
        relay(0, k).start()

    def pass_on(i, carry):
        origin = flip(me, i, ring)
        seq_copy(origin, x_in.at[0], place(here, origin), ss.at[i], rs.at[i]).wait_recv()
        for k in range(1, sides):
            relay(i, k).start()
        return carry

    lax.fori_loop(1, ring, pass_on, 0)

    def sent(i, carry):
        outgoing(i).wait_send()
        return carry

    lax.fori_loop(1, ring, sent, 0)

    def drain(i, carry):
        for k in range(1, sides):
            relay(i, k).wait_send()
            block = place(lax.rem(here - k + sides, sides), flip(me, i, ring))
            side_copy(sides, k, block, block, fs.at[i, k], fr.at[i, k]).wait_recv()
        return carry

    lax.fori_loop(0, ring, drain, 0)
    for load in loads[:3] + loads[9:]:
        load.wait()
    part = rows // share

    def project(c, carry):
        at = rows_at(c * part, part, part)
        flat = context[c].reshape(sides * heads * HD, part)
        total = tokens[at, :].astype(jnp.float32) + lax.dot_general(
            flat, w_out[...].reshape(sides * heads * HD, width), (((0,), (0,)), ((), ())),
            preferred_element_type=jnp.float32,
        )
        hidden[at, :] = total
        normed[at, :] = norm_rows(total, g_ffn[...]).astype(jnp.bfloat16)
        return carry

    lax.fori_loop(0, share, project, 0)
    for load in loads[3:6]:
        load.wait()
    chunk = math.gcd(rows, 128)
    chunks = rows // chunk

    def span(c):
        return rows_at(c * chunk, chunk, chunk)

    def swap(c, k, side):
        return side_copy(
            sides, k, parts.at[side, span(c)], parts.at[side, span(c)], ps.at[c, k], pr.at[c, k]
        )

    def feed(c, carry):
        x = normed[span(c), :]
        gate = jnp.dot(x, up[0], preferred_element_type=jnp.float32)
        lift = jnp.dot(x, up[1], preferred_element_type=jnp.float32)
        active = (jax.nn.gelu(gate, approximate=True) * lift).astype(jnp.bfloat16)
        parts[here, span(c), :] = jnp.dot(
            active, down[...], preferred_element_type=jnp.float32
        ).astype(jnp.bfloat16)
        for k in range(1, sides):
            swap(c, k, here).start()
        return carry

    lax.fori_loop(0, chunks, feed, 0)
    for load in loads[6:9]:
        load.wait()

    def pair_up(c, slot):
        return (
            seq_copy(mate, cross_k.at[slot, span(c)], cross_k.at[slot, span(c)], cs.at[c, 0], cr.at[c, 0]),
            seq_copy(mate, cross_v.at[slot, span(c)], cross_v.at[slot, span(c)], cs.at[c, 1], cr.at[c, 1]),
        )

    def close(c, carry):
        for k in range(1, sides):
            swap(c, k, here).wait_send()
            swap(c, k, lax.rem(here - k + sides, sides)).wait_recv()
        total = hidden[span(c), :]
        for side in range(sides):
            total = total + parts[side, span(c), :].astype(jnp.float32)
        done = norm_rows(total, g_final[...]).astype(jnp.bfloat16)
        encoded[span(c), :] = done
        cross_k[core, span(c), :] = jnp.dot(
            done, w_kv[0], preferred_element_type=jnp.float32
        ).astype(jnp.bfloat16)
        cross_v[core, span(c), :] = jnp.dot(
            done, w_kv[1], preferred_element_type=jnp.float32
        ).astype(jnp.bfloat16)
        for copy in pair_up(c, core):
            copy.start()
        return carry

    lax.fori_loop(0, chunks, close, 0)

    def paired(c, carry):
        for copy in pair_up(c, core):
            copy.wait_send()
        for copy in pair_up(c, 1 - core):
            copy.wait_recv()
        return carry

    lax.fori_loop(0, chunks, paired, 0)
    half = cross_q.shape[0]
    pairs = heads // 2
    peers = ring // 2
    position = lax.broadcasted_iota(jnp.int32, (1, 2 * rows), 1)
    first = me - core
    limit = jnp.where(position < rows, pad_lengths[first], rows + pad_lengths[first + 1])
    bias = jnp.where(position < limit, 0.0, masked_score)
    lane = lax.broadcasted_iota(jnp.int32, (2 * rows, 2 * HD), 1)
    out_lane = lax.broadcasted_iota(jnp.int32, (half, 2 * HD), 1)
    ones = jnp.ones((2 * rows, 2 * HD), jnp.bfloat16)
    stats[...] = jnp.where(out_lane < HD, 0.0, jnp.where(out_lane < HD + heads, 1.0, 0.0))

    def to_peer(i, j):
        to = flip(me, 2 * j, ring)
        source = mixed.at[i, rows_at(lax.div(to, 2) * slab, slab, slab)]
        return seq_copy(to, source, got.at[j, i], ms.at[j, i], mr.at[j, i])

    def to_peers(i):
        def send_one(j, carry):
            to_peer(i, peers - j).start()
            return carry

        lax.fori_loop(1, peers, send_one, 0)

    def cross_pair(i, carry):
        cut = rows_at(i * 2 * HD, 2 * HD, 2 * HD)
        q_here = cross_q[:, cut]
        k_here = cross_k[:, :, cut].reshape(2 * rows, 2 * HD)
        v_here = cross_v[:, :, cut].reshape(2 * rows, 2 * HD)
        pieces = []
        seen = stats[...]
        for h in range(2):
            own = lane < HD if h == 0 else lane >= HD
            keys = jnp.where(own, k_here, jnp.zeros_like(ones))
            values = jnp.where(own, v_here, ones)
            scores = bias + lax.dot_general(
                q_here, keys, (((1,), (1,)), ((), ())), preferred_element_type=jnp.float32
            )
            top = jnp.max(scores, axis=1, keepdims=True)
            weights = jnp.exp(scores - top).astype(jnp.bfloat16)
            piece = jnp.dot(weights, values, preferred_element_type=jnp.float32)
            total = piece[:, 2 * HD - 1 :] if h == 0 else piece[:, :1]
            seen = jnp.where(
                out_lane == 2 * i + h, top, jnp.where(out_lane == HD + 2 * i + h, total, seen)
            )
            pieces.append(piece)
        stats[...] = seen
        mixed[i] = jnp.where(out_lane < HD, pieces[0], pieces[1]).astype(jnp.bfloat16)
        to_peers(i)
        return carry

    lax.fori_loop(0, pairs, cross_pair, 0)
    seen = stats[...]
    high = seen.astype(jnp.bfloat16).astype(jnp.float32)
    rest = seen - high
    middle = rest.astype(jnp.bfloat16).astype(jnp.float32)
    mixed[pairs] = (
        high + pltpu.roll(middle, heads, 1) + pltpu.roll(rest - middle, 2 * heads, 1)
    ).astype(jnp.bfloat16)
    to_peers(pairs)
    got[0] = mixed[:, rows_at(lax.div(me, 2) * slab, slab, slab), :]

    def collect(j, carry):
        for i in range(pairs + 1):
            copy = to_peer(i, j)
            copy.wait_send()
            copy.wait_recv()
        return carry

    lax.fori_loop(1, peers, collect, 0)
    packed = got[:, pairs].astype(jnp.float32).reshape(peers * slab, 2 * HD)
    seen = packed + pltpu.roll(packed, 2 * HD - heads, 1) + pltpu.roll(packed, 2 * HD - 2 * heads, 1)
    sums = pltpu.roll(seen, HD, 1).reshape(peers, slab, 2 * HD)
    seen = seen.reshape(peers, slab, 2 * HD)
    best = jnp.max(seen, axis=0, keepdims=True)
    grow = jnp.exp(seen - best)
    weight_sum = jnp.sum(grow * sums, axis=0, keepdims=True)
    factor = (grow / weight_sum).reshape(peers * slab, 2 * HD)
    factor = jnp.where(lax.broadcasted_iota(jnp.int32, factor.shape, 1) < heads, factor, 0.0)
    column = lax.broadcasted_iota(jnp.int32, (2 * HD, heads * HD), 1)
    row = lax.broadcasted_iota(jnp.int32, (2 * HD, heads * HD), 0)
    spread = jnp.where((column >= row * HD) & (column < row * HD + HD), 1.0, 0.0)
    wide = jnp.dot(
        factor, spread, precision=lax.Precision.HIGHEST, preferred_element_type=jnp.float32
    ).reshape(peers, slab, heads * HD)
    merged = []
    for i in range(pairs):
        weighed = got[:, i].astype(jnp.float32) * wide[:, :, i * 2 * HD : (i + 1) * 2 * HD]
        merged.append(jnp.sum(weighed, axis=0).astype(jnp.bfloat16))
    product = jnp.dot(
        jnp.concatenate(merged, axis=1), w_cross[...], preferred_element_type=jnp.float32
    )
    partial[...] = product.astype(jnp.bfloat16)
    piece = incoming.shape[1]
    divided = piece < slab

    def piece_of(side):
        return rows_at(side * piece, piece, piece) if divided else pl.ds(0, piece)

    def exchange(k, side, origin):
        return side_copy(
            sides, k, partial.at[piece_of(side)], incoming.at[origin], xs.at[k], xr.at[k]
        )

    for k in range(1, sides):
        exchange(k, lax.rem(here + k, sides), here).start()
    incoming[here] = partial[piece_of(here), :]
    for k in range(1, sides):
        exchange(k, lax.rem(here + k, sides), here).wait_send()
        exchange(k, here, lax.rem(here - k + sides, sides)).wait_recv()
    total = incoming[0].astype(jnp.float32)
    for side in range(1, sides):
        total = total + incoming[side].astype(jnp.float32)

    def piece_start(owner, side):
        return slab_start(owner) + (side * piece if divided else 0)

    slot = piece_start(me, here) + lax.broadcasted_iota(jnp.int32, (piece, width), 0)
    limit = jnp.zeros((piece, width), jnp.int32)
    for n in range(target_lengths.shape[0]):
        begun = n * TGT_LEN
        limit = jnp.where(slot >= begun, begun + target_lengths[n], limit)
    decoded[rows_at(piece_start(me, here), piece, piece), :] = (
        mine[piece_of(here), :].astype(jnp.float32) + jnp.where(slot < limit, total, 0.0)
    ).astype(jnp.bfloat16)

    layers = ring // 4

    def block(owner, side):
        return decoded.at[rows_at(piece_start(owner, side), piece, piece)]

    def near(n):
        return flip(me, 2 * n, ring)

    def to_layer(m, owner):
        return seq_copy(flip(me, 4 * m, ring), block(owner, here), block(owner, here), zs.at[m], zr.at[m])

    def to_row(m, owner):
        return seq_copy(flip(me, 2, ring), block(owner, here), block(owner, here), ys.at[m], yr.at[m])

    def to_side(k, n, side):
        return side_copy(
            sides, k, block(near(n), side), block(near(n), side), ws.at[k, n], wr.at[k, n]
        )

    def to_mate(k, owner):
        def at(n):
            side = lax.rem(here - k + sides, sides)
            source = block(flip(owner, 2 * n, ring), side)
            return seq_copy(mate, source, source, hs.at[k, n], hr.at[k, n])

        return at

    given = range(1, sides) if divided else ()

    def pass_block(n):
        for k in given:
            to_side(k, n, here).start()
        to_mate(0, me)(n).start()

    for m in range(layers - 1, 0, -1):
        to_layer(m, me).start()
    to_row(0, me).start()
    pass_block(0)
    for m in range(layers):
        if m:
            to_layer(m, near(2 * m)).wait_recv()
            to_row(m, near(2 * m)).start()
            pass_block(2 * m)
        to_row(m, near(2 * m + 1)).wait_recv()
        pass_block(2 * m + 1)

    def across(n, carry):
        for k in given:
            to_side(k, n, lax.rem(here - k + sides, sides)).wait_recv()
            to_mate(k, me)(n).start()
        return carry

    lax.fori_loop(0, peers, across, 0)
    for m in range(layers):
        if m:
            to_layer(m, me).wait_send()
        to_row(m, near(2 * m)).wait_send()

    def settle(n, carry):
        for k in given:
            to_side(k, n, here).wait_send()
        for k in (0, *given):
            to_mate(k, me)(n).wait_send()
            to_mate(k, mate)(n).wait_recv()
        return carry

    lax.fori_loop(0, peers, settle, 0)


def encoder_block(
    ring, share, sides, back, pad_lengths, target_lengths, tokens, g_ffn, g_final, w_own, w_all,
    ffn_in, ffn_out, w_kv, cross_q, w_cross, targets,
):
    rows, width = tokens.shape
    heads = ring // share
    chunks = rows // math.gcd(rows, 128)
    slab = targets.shape[0] // ring
    piece = slab // sides if slab % (16 * sides) == 0 else slab
    half, lanes = cross_q.shape
    pairs = heads // 2
    peers = ring // 2
    layers = ring // 4
    bf16 = jnp.bfloat16
    vmem = pl.BlockSpec(memory_space=pltpu.VMEM)
    smem = pl.BlockSpec(memory_space=pltpu.SMEM)
    hbm = pl.BlockSpec(memory_space=pltpu.HBM)
    dma = pltpu.SemaphoreType.DMA
    return pl.pallas_call(
        functools.partial(block_kernel, ring, share, sides),
        out_shape=(
            jax.ShapeDtypeStruct((rows, width), bf16),
            jax.ShapeDtypeStruct(targets.shape, bf16),
        ),
        in_specs=[vmem, smem, smem] + [hbm] * 8 + [vmem, hbm, hbm],
        out_specs=(vmem, vmem),
        scratch_shapes=[
            pltpu.VMEM((rows, width), bf16),
            pltpu.VMEM((1, width), jnp.float32),
            pltpu.VMEM((1, width), jnp.float32),
            pltpu.VMEM((sides,) + w_own.shape, bf16),
            pltpu.VMEM((share, sides * heads, HD, rows // share), bf16),
            pltpu.VMEM((rows, width), jnp.float32),
            pltpu.VMEM((rows, width), bf16),
            pltpu.VMEM((sides, rows, width), bf16),
            pltpu.VMEM(ffn_in.shape, bf16),
            pltpu.VMEM(ffn_out.shape, bf16),
            pltpu.VMEM(w_kv.shape, bf16),
            pltpu.VMEM(w_cross.shape, bf16),
            pltpu.VMEM((slab, width), bf16),
            pltpu.VMEM((2, rows, lanes), bf16),
            pltpu.VMEM((2, rows, lanes), bf16),
            pltpu.VMEM((pairs + 1, half, 2 * HD), bf16),
            pltpu.VMEM((half, 2 * HD), jnp.float32),
            pltpu.VMEM((peers, pairs + 1, slab, 2 * HD), bf16),
            pltpu.VMEM((slab, width), bf16),
            pltpu.VMEM((sides, piece, width), bf16),
            dma((9 + sides,)),
            dma((ring,)),
            dma((ring,)),
            dma((ring, sides)),
            dma((ring, sides)),
            dma((chunks, sides)),
            dma((chunks, sides)),
            dma((chunks, 2)),
            dma((chunks, 2)),
            dma((peers, pairs + 1)),
            dma((peers, pairs + 1)),
            dma((sides,)),
            dma((sides,)),
            dma((layers,)),
            dma((layers,)),
            dma((layers,)),
            dma((layers,)),
            dma((sides, peers)),
            dma((sides, peers)),
            dma((sides, peers)),
            dma((sides, peers)),
        ],
        compiler_params=pltpu.CompilerParams(
            collective_id=1, has_side_effects=True, vmem_limit_bytes=50 * 1024 * 1024
        ),
        name="encoder_block",
    )(
        back, pad_lengths, target_lengths, tokens, g_ffn[None, :], g_final[None, :], w_own, w_all,
        ffn_in, ffn_out, w_kv, cross_q, w_cross, targets,
    )


def attend_kernel(lengths, q_ref, kv_ref, o_ref, keys, values, flipped, count):
    blocks, span, lanes = kv_ref.shape
    tile = span
    queries = q_ref.shape[1]
    group = math.gcd(queries, 256)
    ones_rows = flipped.shape[1] - HD
    lane = lax.broadcasted_iota(jnp.int32, (span, lanes), 1)
    row = lax.broadcasted_iota(jnp.int32, (span, lanes), 0)

    @pl.when(pl.program_id(0) == 0)
    def pack():
        def place(j, start):
            block = kv_ref[j]
            dead = jnp.where(row < lengths[j], 0.0, masked_score).astype(jnp.bfloat16)
            at = pl.ds(pl.multiple_of(start, 16), span)
            keys[at, :] = jnp.where(lane < HD, block, dead)
            values[at, :] = jnp.where(lane < HD, jnp.ones_like(block), block)
            return start + ((lengths[j] + 15) // 16) * 16

        stop = lax.fori_loop(0, blocks, place, 0)
        at = pl.ds(pl.multiple_of(stop, 16), span)
        keys[at, :] = jnp.where(lane < HD, 0.0, masked_score).astype(jnp.bfloat16)
        values[at, :] = jnp.zeros((span, lanes), jnp.bfloat16)
        count[0] = (stop + tile - 1) // tile

        def flip(t, carry):
            at = pl.ds(pl.multiple_of(t * tile, tile), tile)
            flipped[t] = values[at, :].T[HD - ones_rows :, :]
            return carry

        lax.fori_loop(0, count[0], flip, 0)

    spare = lax.broadcasted_iota(jnp.int32, (HD, queries), 0)
    pick = jnp.where(spare == 0, 1.0, 0.0).astype(jnp.bfloat16)
    q_wide = jnp.concatenate([q_ref[...], pick], axis=0)
    cuts = [slice(g, g + group) for g in range(0, queries, group)]

    def step(t, state):
        at = pl.ds(pl.multiple_of(t * tile, tile), tile)
        keys_here = keys[at, :]
        values_here = flipped[t]
        all_scores = [
            jnp.dot(keys_here, q_wide[:, cut], preferred_element_type=jnp.float32) for cut in cuts
        ]
        updated = []
        for scores, (top, mixed) in zip(all_scores, state):
            new_top = jnp.maximum(top, jnp.max(scores, axis=0, keepdims=True))
            weights = jnp.exp(scores - new_top).astype(jnp.bfloat16)
            part = jnp.dot(values_here, weights, preferred_element_type=jnp.float32)
            updated.append((new_top, mixed * jnp.exp(top - new_top) + part))
        return tuple(updated)

    start = tuple(
        (
            jnp.full((1, group), masked_score, jnp.float32),
            jnp.zeros((ones_rows + HD, group), jnp.float32),
        )
        for cut in cuts
    )
    ends = lax.fori_loop(0, count[0], step, start)
    for cut, (top, mixed) in zip(cuts, ends):
        o_ref[:, cut] = (mixed[ones_rows:, :] / mixed[0:1, :]).astype(jnp.bfloat16)


def attend(q_all, kv_all, pad_lengths):
    blocks, span, lanes = kv_all.shape
    total = q_all.shape[1]
    width = math.gcd(total, 2048)
    return pl.pallas_call(
        attend_kernel,
        out_shape=jax.ShapeDtypeStruct((HD, total), jnp.bfloat16),
        grid_spec=pltpu.PrefetchScalarGridSpec(
            num_scalar_prefetch=1,
            grid=(total // width,),
            in_specs=[
                pl.BlockSpec((HD, width), lambda i, lengths: (0, i)),
                pl.BlockSpec((blocks, span, lanes), lambda i, lengths: (0, 0, 0)),
            ],
            out_specs=pl.BlockSpec((HD, width), lambda i, lengths: (0, i)),
            scratch_shapes=[
                pltpu.VMEM(((blocks + 1) * span, lanes), jnp.bfloat16),
                pltpu.VMEM(((blocks + 1) * span, lanes), jnp.bfloat16),
                pltpu.VMEM((blocks + 1, HD + 16, span), jnp.bfloat16),
                pltpu.SMEM((1,), jnp.int32),
            ],
        ),
        compiler_params=pltpu.CompilerParams(
            dimension_semantics=("arbitrary",), vmem_limit_bytes=48 * 1024 * 1024
        ),
        name="attend",
    )(pad_lengths, q_all, kv_all)


def local(
    ring,
    sides,
    tokens,
    norm_attn,
    self_qkv,
    self_out,
    norm_ffn,
    ffn_in,
    ffn_out,
    norm_final,
    pad_lengths,
    targets,
    target_lengths,
    norm_cross,
    cross_query,
    cross_kv,
    cross_out,
):
    heads_here = self_qkv.shape[2] // HD
    share = ring // heads_here
    part = tokens.shape[0] // share
    q_got, kv_got, out_all, cross_q = scatter_heads(
        ring, share, sides, tokens, norm_attn, self_qkv, self_out, targets, norm_cross, cross_query
    )
    q_all = q_got.transpose(1, 0, 2).reshape(HD, ring * part)
    mixed_t = attend(q_all, kv_got, pad_lengths)
    back = mixed_t.reshape(HD, ring, part).transpose(1, 0, 2)
    return encoder_block(
        ring,
        share,
        sides,
        back,
        pad_lengths,
        target_lengths,
        tokens,
        norm_ffn,
        norm_final,
        self_out,
        out_all,
        ffn_in,
        ffn_out,
        cross_kv,
        cross_q,
        cross_out,
        targets,
    )


def solution(mesh):
    ring = mesh.shape["seq"]
    sides = mesh.shape["head"]
    placed = (
        P("seq", None),
        P(),
        P(None, None, "head"),
        P("head", None),
        P(),
        P(None, None, "head"),
        P("head", None),
        P(),
        P(),
        P(),
        P(),
        P(),
        P(None, "head"),
        P(None, None, "head"),
        P("head", None),
    )
    return jax.shard_map(
        functools.partial(local, ring, sides),
        mesh=mesh,
        in_specs=placed,
        out_specs=(P("seq", None), P()),
        check_vma=False,
    )
```

time: 182 us -> 171 us (0.940)
  Pallas kernels: 172 us -> 159 us
  local copies, waits for them, and re-layouts: 7.85 us -> 11.5 us
    pallas_call x1, Pallas kernels: 102 us -> 85.1 us  [encoder_block(): pl.pallas_call(functools.partial(block_kernel, ring, share, sides), out_s...]
    pallas_call x1, Pallas kernels: 33.5 us -> 45.6 us  [scatter_heads(): pl.pallas_call(functools.partial(scatter_kernel, ring, share, sides), out...]
    pallas_call x1, Pallas kernels: 34.3 us -> 27.9 us  [attend(): pl.pallas_call(attend_kernel, out_shape=jax.ShapeDtypeStruct((HD, total),...]
    unnamed x26 -> x28, local copies, waits for them, and re-layouts: 7.09 us -> 11.4 us
    pallas_call x1 -> x0, Pallas kernels: 2.17 us -> none  [project_heads(): pl.pallas_call(functools.partial(project_kernel, share), out_shape=(jax.S...]
where the time goes in v1:
time: 171 us
  Pallas kernels  159 us (93%)
  local copies, waits for them, and re-layouts  11.5 us (7%)
    pallas_call x1, Pallas kernels, encoder_block(): pl.pallas_call(functools.partial(block_kernel, ring, share, sides), out_s...  85.1 us
    pallas_call x1, Pallas kernels, scatter_heads(): pl.pallas_call(functools.partial(scatter_kernel, ring, share, sides), out...  45.6 us
    pallas_call x1, Pallas kernels, attend(): pl.pallas_call(attend_kernel, out_shape=jax.ShapeDtypeStruct((HD, total),...  27.9 us
    unnamed x28, local copies, waits for them, and re-layouts  11.4 us

profile of v1, /device:TPU:0, one launch (start us, length us, event | category | flops | bytes accessed | tf_op | source)
XLA Modules:
  0.0 170.9 jit_solution(18331638794100274363)
XLA Ops:
  0.6 0.0 copy-start
  0.6 1.2 copy-done
  1.9 0.0 copy-start.2
  1.9 1.2 copy-done.2
  3.1 0.0 copy-start.3
  3.1 1.2 copy-done.3
  4.3 0.0 copy-start.4
  4.3 1.9 %copy-done.4 = bf16[3,1024,512]{2,1,0:T(8,128)(2,1)S(1)} copy-done((bf16[3,1024,512]{2,1,0:T(8,128)(2,1)S(1)}, bf16[3,1024,512]{2,1,0:T(8,128)(2,1)}, u32[]{:S(2)}) %copy-start.4) | copy-done | bytes 3145752
  6.2 0.0 copy-start.6
  6.2 1.2 copy-done.6
  7.4 0.0 copy-start.7
  7.4 0.7 copy-done.7
  8.1 0.0 copy-start.8
  8.1 0.7 copy-done.8
  8.8 0.0 copy-start.11
  8.8 45.6 %scatter_heads.1 = (bf16[16,64,256]{2,1,0:T(8,128)(2,1)S(1)}, bf16[16,512,128]{2,1,0:T(8,128)(2,1)S(1)}, bf16[2,512,1024]{2,1,0:T(8,128)(2,1)S(1)}, bf16[256,512]{1,0:T(8,128)(2,1)S(1)}) custom-call(bf16[512,1024]{1,0:T(8,128)(2,1)S(1)} %copy-done, f32[1,1024]{1,0:T(1,128)S(1)} %bitcast.18, bf16[3,1024,512]{2,1,0:T(8,128)(2,1)S(1)} %copy-done.4, ...), custom_call_target="tpu_custom_call" | custom-call | tf_op jit(solution)/shard_map/scatter_heads/pallas_call | solution.py:219
  54.4 0.0 copy-start.5
  54.5 1.3 copy-done.5
  55.8 0.0 copy-start.1
  55.8 0.0 copy-start.9
  55.8 0.0 copy-start.10
  55.8 0.0 copy-start.12
  55.8 0.0 copy-done.11
  55.8 27.9 %attend.1 = bf16[64,4096]{1,0:T(8,128)(2,1)S(1)} custom-call(s32[16]{0:T(128)S(1)} %copy-done.11, bf16[64,4096]{1,0:T(8,128)(2,1)S(1)} %bitcast.15, bf16[16,512,128]{2,1,0:T(8,128)(2,1)S(1)} %get-tuple-element.7.kv_ref), custom_call_target="tpu_custom_call" | custom-call | tf_op jit(solution)/shard_map/attend/pallas_call | solution.py:768
  83.8 0.0 copy-done.1
  83.8 0.0 copy-done.9
  83.8 0.0 copy-done.10
  83.8 0.0 copy-done.12
  83.8 85.1 %encoder_block.1 = (bf16[512,1024]{1,0:T(8,128)(2,1)S(1)}, bf16[512,1024]{1,0:T(8,128)(2,1)S(1)}) custom-call(bf16[16,64,256]{2,1,0:T(8,128)(2,1)S(1)} %bitcast.14, s32[16]{0:T(128)S(1)} %copy-done.11, s32[4]{0:T(128)S(1)} %copy-done.12, bf16[512,1024]{1,0:T(8,128)(2,1)S(1)} %copy-done.1, f32[1,1024]{1,0:T(1,128)S(1)} %bitcast.20, f32[1,1024]{1,0:T(1,128)S(1)} %bitcast.21, ...), custom_call_target="tpu_custom_call" | custom-call | tf_op jit(solution)/shard_map/encoder_block/pallas_call | solution.py:639
  168.9 1.0 copy.26
  169.9 1.0 copy.27
  (2 shorter events, 0.1 us)
Async XLA Ops:
  0.6 1.2 copy-start
  1.9 1.2 copy-start.2
  3.1 1.2 copy-start.3
  4.3 1.9 %copy-start.4 = (bf16[3,1024,512]{2,1,0:T(8,128)(2,1)S(1)}, bf16[3,1024,512]{2,1,0:T(8,128)(2,1)}, u32[]{:S(2)}) copy-start(bf16[3,1024,512]{2,1,0:T(8,128)(2,1)} %qkv_hbm.1) | copy-start | bytes 9437188
  6.2 1.2 copy-start.6
  7.4 0.7 copy-start.7
  8.1 0.7 copy-start.8
  8.8 47.0 %copy-start.11 = (s32[16]{0:T(128)S(1)}, s32[16]{0:T(128)}, u32[]{:S(2)}) copy-start(s32[16]{0:T(128)} %pad_lengths.1) | copy-start | bytes 196
  54.4 1.3 copy-start.5
  55.8 28.0 %copy-start.1 = (bf16[512,1024]{1,0:T(8,128)(2,1)S(1)}, bf16[512,1024]{1,0:T(8,128)(2,1)}, u32[]{:S(2)}) copy-start(bf16[512,1024]{1,0:T(8,128)(2,1)} %tokens_hbm.3) | copy-start | bytes 3145732
  55.8 28.0 %copy-start.9 = (f32[1024]{0:T(1024)S(1)}, f32[1024]{0:T(1024)}, u32[]{:S(2)}) copy-start(f32[1024]{0:T(1024)} %param.19) | copy-start | bytes 12292
  55.8 28.0 %copy-start.10 = (f32[1024]{0:T(1024)S(1)}, f32[1024]{0:T(1024)}, u32[]{:S(2)}) copy-start(f32[1024]{0:T(1024)} %param.22) | copy-start | bytes 12292
  55.8 28.0 %copy-start.12 = (s32[4]{0:T(128)S(1)}, s32[4]{0:T(128)}, u32[]{:S(2)}) copy-start(s32[4]{0:T(128)} %target_lengths.1) | copy-start | bytes 52

commit v2 on v1

--- a/solution.py
+++ b/solution.py
@@ -70,6 +70,10 @@
         device_id={"head": lax.rem(here + k, sides)},
         device_id_type=MESH,
     )
+
+
+def in_hbm(array):
+    return pltpu.with_memory_space_constraint(array, pltpu.HBM)
 
 
 def norm_rows(values, gain):
@@ -144,11 +148,22 @@
         for s in range(share):
             kv_in[h * share + s] = both[s * part : (s + 1) * part, :]
 
-    def send_kv(i, carry):
-        kv_copy(ring - i).start()
-        return carry
-
-    lax.fori_loop(1, ring, send_kv, 0)
+    span = ring // 2
+    inner = lax.rem(lax.div(me, span) + lax.div(me, ring // 4), 2)
+
+    def send_half(copy, far):
+        def send(n, carry):
+            step = far * span + n
+
+            @pl.when(step > 0)
+            def away():
+                copy(step).start()
+
+            return carry
+
+        lax.fori_loop(0, span, send, 0)
+
+    send_half(kv_copy, inner)
     own_kv = pltpu.make_async_copy(kv_in.at[me], kv_out.at[me, mine], os.at[1])
     own_kv.start()
     loads[4].wait()
@@ -159,11 +174,9 @@
         for s in range(share):
             q_in[h * share + s] = queries[h * HD : (h + 1) * HD, s * part : (s + 1) * part]
 
-    def send_q(i, carry):
-        q_copy(ring - i).start()
-        return carry
-
-    lax.fori_loop(1, ring, send_q, 0)
+    send_half(q_copy, 0)
+    send_half(kv_copy, 1 - inner)
+    send_half(q_copy, 1)
     own_q = pltpu.make_async_copy(q_in.at[me], q_out.at[me], os.at[0])
     own_q.start()
     own_kv.wait()
@@ -251,7 +264,7 @@
             collective_id=0, has_side_effects=True, vmem_limit_bytes=40 * 1024 * 1024
         ),
         name="scatter_heads",
-    )(tokens, gain[None, :], qkv, w_out, targets, g_cross[None, :], w_cross)
+    )(*map(in_hbm, (tokens, gain[None, :], qkv, w_out, targets, g_cross[None, :], w_cross)))
 
 
 def block_kernel(
@@ -312,7 +325,7 @@
         return side_copy(sides, k, block, block, fs.at[i, k], fr.at[i, k])
 
     def send(i, carry):
-        outgoing(ring - i).start()
+        outgoing(i).start()
         return carry
 
     lax.fori_loop(1, ring, send, 0)
@@ -784,7 +797,7 @@
             ],
         ),
         compiler_params=pltpu.CompilerParams(
-            dimension_semantics=("arbitrary",), vmem_limit_bytes=48 * 1024 * 1024
+            dimension_semantics=("arbitrary",), vmem_limit_bytes=32 * 1024 * 1024
         ),
         name="attend",
     )(pad_lengths, q_all, kv_all)

time: 171 us -> 160 us (0.936); the launches traced: 171 us -> 163 us
  local copies, waits for them, and re-layouts: 11.5 us -> 2.06 us
    unnamed x28 -> x14, local copies, waits for them, and re-layouts: 11.4 us -> 1.98 us
    pallas_call x1, Pallas kernels: 27.9 us -> 34.3 us  [attend(): pl.pallas_call(attend_kernel, out_shape=jax.ShapeDtypeStruct((HD, total),...]
    pallas_call x1, Pallas kernels: 45.6 us -> 41.8 us  [scatter_heads(): pl.pallas_call(functools.partial(scatter_kernel, ring, share, sides), out...]
where the time goes in v2:
time: 160 us; the launch traced here: 163 us
  Pallas kernels  160 us (100%)
  local copies, waits for them, and re-layouts  2.06 us (1%)
    pallas_call x1, Pallas kernels, encoder_block(): pl.pallas_call(functools.partial(block_kernel, ring, share, sides), out_s...  83.8 us
    pallas_call x1, Pallas kernels, scatter_heads(): pl.pallas_call(functools.partial(scatter_kernel, ring, share, sides), out...  41.8 us
    pallas_call x1, Pallas kernels, attend(): pl.pallas_call(attend_kernel, out_shape=jax.ShapeDtypeStruct((HD, total),...  34.3 us

profile of v2, /device:TPU:0, one launch (start us, length us, event | category | flops | bytes accessed | tf_op | source)
XLA Modules:
  0.0 162.7 jit_solution(12287852403675365541)
XLA Ops:
  0.6 0.0 copy-start.4
  0.6 41.8 %scatter_heads.1 = (bf16[16,64,256]{2,1,0:T(8,128)(2,1)S(1)}, bf16[16,512,128]{2,1,0:T(8,128)(2,1)S(1)}, bf16[2,512,1024]{2,1,0:T(8,128)(2,1)S(1)}, bf16[256,512]{1,0:T(8,128)(2,1)S(1)}) custom-call(bf16[512,1024]{1,0:T(8,128)(2,1)} %tokens_hbm.3, f32[1,1024]{1,0:T(1,128)} %bitcast.20, bf16[3,1024,512]{2,1,0:T(8,128)(2,1)} %qkv_hbm.1, ...), custom_call_target="tpu_custom_call" | custom-call | tf_op jit(solution)/shard_map/scatter_heads/pallas_call | solution.py:232
  42.4 0.0 copy-start.1
  42.5 0.0 copy-start
  42.5 0.0 copy-start.2
  42.5 0.0 copy-start.3
  42.5 0.0 copy-start.5
  42.5 0.0 copy-done.4
  42.6 34.3 %attend.1 = bf16[64,4096]{1,0:T(8,128)(2,1)S(1)} custom-call(s32[16]{0:T(128)S(1)} %copy-done.4, bf16[64,4096]{1,0:T(8,128)(2,1)S(1)} %bitcast.15, bf16[16,512,128]{2,1,0:T(8,128)(2,1)S(1)} %get-tuple-element.7.kv_ref), custom_call_target="tpu_custom_call" | custom-call | tf_op jit(solution)/shard_map/attend/pallas_call | solution.py:781
  76.9 0.0 copy-done.1
  76.9 0.0 copy-done
  76.9 0.0 copy-done.2
  76.9 0.0 copy-done.3
  76.9 0.0 copy-done.5
  76.9 83.8 %encoder_block.1 = (bf16[512,1024]{1,0:T(8,128)(2,1)S(1)}, bf16[512,1024]{1,0:T(8,128)(2,1)S(1)}) custom-call(bf16[16,64,256]{2,1,0:T(8,128)(2,1)S(1)} %bitcast.14, s32[16]{0:T(128)S(1)} %copy-done.4, s32[4]{0:T(128)S(1)} %copy-done.5, bf16[512,1024]{1,0:T(8,128)(2,1)S(1)} %copy-done, f32[1,1024]{1,0:T(1,128)S(1)} %bitcast.18, f32[1,1024]{1,0:T(1,128)S(1)} %bitcast.19, ...), custom_call_target="tpu_custom_call" | custom-call | tf_op jit(solution)/shard_map/encoder_block/pallas_call | solution.py:652
  160.7 1.0 copy.26
  161.7 1.0 copy.27
  (2 shorter events, 0.1 us)
Async XLA Ops:
  0.6 41.9 %copy-start.4 = (s32[16]{0:T(128)S(1)}, s32[16]{0:T(128)}, u32[]{:S(2)}) copy-start(s32[16]{0:T(128)} %pad_lengths.1) | copy-start | bytes 196
  42.4 34.4 %copy-start.1 = (bf16[2,512,1024]{2,1,0:T(8,128)(2,1)}, bf16[2,512,1024]{2,1,0:T(8,128)(2,1)S(1)}, u32[]{:S(2)}) copy-start(bf16[2,512,1024]{2,1,0:T(8,128)(2,1)S(1)} %get-tuple-element.8.w_all_hbm) | copy-start | bytes 6291460
  42.5 34.4 %copy-start = (bf16[512,1024]{1,0:T(8,128)(2,1)S(1)}, bf16[512,1024]{1,0:T(8,128)(2,1)}, u32[]{:S(2)}) copy-start(bf16[512,1024]{1,0:T(8,128)(2,1)} %tokens_hbm.3) | copy-start | bytes 3145732
  42.5 34.4 %copy-start.2 = (f32[1024]{0:T(1024)S(1)}, f32[1024]{0:T(1024)}, u32[]{:S(2)}) copy-start(f32[1024]{0:T(1024)} %param.19) | copy-start | bytes 12292
  42.5 34.4 %copy-start.3 = (f32[1024]{0:T(1024)S(1)}, f32[1024]{0:T(1024)}, u32[]{:S(2)}) copy-start(f32[1024]{0:T(1024)} %param.22) | copy-start | bytes 12292
  42.5 34.4 %copy-start.5 = (s32[4]{0:T(128)S(1)}, s32[4]{0:T(128)}, u32[]{:S(2)}) copy-start(s32[4]{0:T(128)} %target_lengths.1) | copy-start | bytes 52

commit v3 on v2

--- a/solution.py
+++ b/solution.py
@@ -13,6 +13,7 @@
 
 epsilon = 1e-06
 masked_score = -1e30
+scaling = HD ** (-0.5) * math.log2(math.e)
 MESH = pl.DeviceIdType.MESH
 
 
@@ -167,9 +168,12 @@
     own_kv = pltpu.make_async_copy(kv_in.at[me], kv_out.at[me, mine], os.at[1])
     own_kv.start()
     loads[4].wait()
-    queries = lax.dot_general(
-        qkv[0], normed[...], (((0,), (1,)), ((), ())), preferred_element_type=jnp.float32
-    ).astype(jnp.bfloat16) * jnp.bfloat16(HD ** (-0.5))
+    queries = (
+        lax.dot_general(
+            qkv[0], normed[...], (((0,), (1,)), ((), ())), preferred_element_type=jnp.float32
+        )
+        * scaling
+    ).astype(jnp.bfloat16)
     for h in range(heads):
         for s in range(share):
             q_in[h * share + s] = queries[h * HD : (h + 1) * HD, s * part : (s + 1) * part]
@@ -185,9 +189,9 @@
     for load in loads[5:]:
         load.wait()
     cross_normed = norm_rows(targets[...].astype(jnp.float32), g_cross[...]).astype(jnp.bfloat16)
-    cross_q[...] = jnp.dot(
-        cross_normed, w_cross[...], preferred_element_type=jnp.float32
-    ).astype(jnp.bfloat16) * jnp.bfloat16(HD ** (-0.5))
+    cross_q[...] = (
+        jnp.dot(cross_normed, w_cross[...], preferred_element_type=jnp.float32) * scaling
+    ).astype(jnp.bfloat16)
 
     def relay(i, carry):
         origin = flip(me, i, ring)
@@ -273,7 +277,7 @@
     encoded, decoded,
     tokens, g_ffn, g_final, w_out, context, hidden, normed, parts, up, down, w_kv, w_cross, mine,
     cross_k, cross_v, mixed, stats, got, partial, incoming,
-    ls, ss, rs, fs, fr, ps, pr, cs, cr, ms, mr, xs, xr, zs, zr, ys, yr, ws, wr, hs, hr,
+    ls, ss, rs, fs, fr, ps, pr, cs, cr, ms, mr, xs, xr, zs, zr, ws, wr, hs, hr,
 ):
     me = lax.axis_index("seq")
     here = lax.axis_index("head")
@@ -439,10 +443,10 @@
     half = cross_q.shape[0]
     pairs = heads // 2
     peers = ring // 2
-    position = lax.broadcasted_iota(jnp.int32, (1, 2 * rows), 1)
+    position = lax.broadcasted_iota(jnp.int32, (2 * rows, 2 * HD), 0)
     first = me - core
     limit = jnp.where(position < rows, pad_lengths[first], rows + pad_lengths[first + 1])
-    bias = jnp.where(position < limit, 0.0, masked_score)
+    dead = jnp.where(position < limit, 0.0, masked_score).astype(jnp.bfloat16)
     lane = lax.broadcasted_iota(jnp.int32, (2 * rows, 2 * HD), 1)
     out_lane = lax.broadcasted_iota(jnp.int32, (half, 2 * HD), 1)
     ones = jnp.ones((2 * rows, 2 * HD), jnp.bfloat16)
@@ -469,13 +473,15 @@
         seen = stats[...]
         for h in range(2):
             own = lane < HD if h == 0 else lane >= HD
-            keys = jnp.where(own, k_here, jnp.zeros_like(ones))
+            keys = jnp.where(own, k_here, dead)
             values = jnp.where(own, v_here, ones)
-            scores = bias + lax.dot_general(
-                q_here, keys, (((1,), (1,)), ((), ())), preferred_element_type=jnp.float32
+            pick = jnp.where(out_lane == (HD if h == 0 else 0), 1.0, 0.0).astype(jnp.bfloat16)
+            queries = jnp.where(out_lane < HD if h == 0 else out_lane >= HD, q_here, pick)
+            scores = lax.dot_general(
+                queries, keys, (((1,), (1,)), ((), ())), preferred_element_type=jnp.float32
             )
             top = jnp.max(scores, axis=1, keepdims=True)
-            weights = jnp.exp(scores - top).astype(jnp.bfloat16)
+            weights = jnp.exp2(scores - top).astype(jnp.bfloat16)
             piece = jnp.dot(weights, values, preferred_element_type=jnp.float32)
             total = piece[:, 2 * HD - 1 :] if h == 0 else piece[:, :1]
             seen = jnp.where(
@@ -511,7 +517,7 @@
     sums = pltpu.roll(seen, HD, 1).reshape(peers, slab, 2 * HD)
     seen = seen.reshape(peers, slab, 2 * HD)
     best = jnp.max(seen, axis=0, keepdims=True)
-    grow = jnp.exp(seen - best)
+    grow = jnp.exp2(seen - best)
     weight_sum = jnp.sum(grow * sums, axis=0, keepdims=True)
     factor = (grow / weight_sum).reshape(peers * slab, 2 * HD)
     factor = jnp.where(lax.broadcasted_iota(jnp.int32, factor.shape, 1) < heads, factor, 0.0)
@@ -562,70 +568,66 @@
         mine[piece_of(here), :].astype(jnp.float32) + jnp.where(slot < limit, total, 0.0)
     ).astype(jnp.bfloat16)
 
-    layers = ring // 4
-
     def block(owner, side):
         return decoded.at[rows_at(piece_start(owner, side), piece, piece)]
 
     def near(n):
         return flip(me, 2 * n, ring)
 
-    def to_layer(m, owner):
-        return seq_copy(flip(me, 4 * m, ring), block(owner, here), block(owner, here), zs.at[m], zr.at[m])
-
-    def to_row(m, owner):
-        return seq_copy(flip(me, 2, ring), block(owner, here), block(owner, here), ys.at[m], yr.at[m])
+    def to_near(n, owner):
+        return seq_copy(near(n), block(owner, here), block(owner, here), zs.at[n], zr.at[n])
 
     def to_side(k, n, side):
         return side_copy(
             sides, k, block(near(n), side), block(near(n), side), ws.at[k, n], wr.at[k, n]
         )
 
-    def to_mate(k, owner):
-        def at(n):
-            side = lax.rem(here - k + sides, sides)
-            source = block(flip(owner, 2 * n, ring), side)
-            return seq_copy(mate, source, source, hs.at[k, n], hr.at[k, n])
-
-        return at
+    def to_mate(k, n, owner):
+        side = lax.rem(here - k + sides, sides)
+        source = block(flip(owner, 2 * n, ring), side)
+        return seq_copy(mate, source, source, hs.at[k, n], hr.at[k, n])
 
     given = range(1, sides) if divided else ()
+
+    def share_out(n, carry):
+        to_near(n, me).start()
+        return carry
+
+    lax.fori_loop(1, peers, share_out, 0)
 
     def pass_block(n):
         for k in given:
             to_side(k, n, here).start()
-        to_mate(0, me)(n).start()
-
-    for m in range(layers - 1, 0, -1):
-        to_layer(m, me).start()
-    to_row(0, me).start()
+        to_mate(0, n, me).start()
+
     pass_block(0)
-    for m in range(layers):
-        if m:
-            to_layer(m, near(2 * m)).wait_recv()
-            to_row(m, near(2 * m)).start()
-            pass_block(2 * m)
-        to_row(m, near(2 * m + 1)).wait_recv()
-        pass_block(2 * m + 1)
+
+    def pass_along(n, carry):
+        to_near(n, near(n)).wait_recv()
+        pass_block(n)
+        return carry
+
+    lax.fori_loop(1, peers, pass_along, 0)
 
     def across(n, carry):
         for k in given:
             to_side(k, n, lax.rem(here - k + sides, sides)).wait_recv()
-            to_mate(k, me)(n).start()
+            to_mate(k, n, me).start()
         return carry
 
     lax.fori_loop(0, peers, across, 0)
-    for m in range(layers):
-        if m:
-            to_layer(m, me).wait_send()
-        to_row(m, near(2 * m)).wait_send()
+    def spent(n, carry):
+        to_near(n, me).wait_send()
+        return carry
+
+    lax.fori_loop(1, peers, spent, 0)
 
     def settle(n, carry):
         for k in given:
             to_side(k, n, here).wait_send()
         for k in (0, *given):
-            to_mate(k, me)(n).wait_send()
-            to_mate(k, mate)(n).wait_recv()
+            to_mate(k, n, me).wait_send()
+            to_mate(k, n, mate).wait_recv()
         return carry
 
     lax.fori_loop(0, peers, settle, 0)
@@ -643,7 +645,6 @@
     half, lanes = cross_q.shape
     pairs = heads // 2
     peers = ring // 2
-    layers = ring // 4
     bf16 = jnp.bfloat16
     vmem = pl.BlockSpec(memory_space=pltpu.VMEM)
     smem = pl.BlockSpec(memory_space=pltpu.SMEM)
@@ -691,10 +692,8 @@
             dma((peers, pairs + 1)),
             dma((sides,)),
             dma((sides,)),
-            dma((layers,)),
-            dma((layers,)),
-            dma((layers,)),
-            dma((layers,)),
+            dma((peers,)),
+            dma((peers,)),
             dma((sides, peers)),
             dma((sides, peers)),
             dma((sides, peers)),
@@ -757,9 +756,9 @@
         updated = []
         for scores, (top, mixed) in zip(all_scores, state):
             new_top = jnp.maximum(top, jnp.max(scores, axis=0, keepdims=True))
-            weights = jnp.exp(scores - new_top).astype(jnp.bfloat16)
+            weights = jnp.exp2(scores - new_top).astype(jnp.bfloat16)
             part = jnp.dot(values_here, weights, preferred_element_type=jnp.float32)
-            updated.append((new_top, mixed * jnp.exp(top - new_top) + part))
+            updated.append((new_top, mixed * jnp.exp2(top - new_top) + part))
         return tuple(updated)
 
     start = tuple(
@@ -777,7 +776,7 @@
 def attend(q_all, kv_all, pad_lengths):
     blocks, span, lanes = kv_all.shape
     total = q_all.shape[1]
-    width = math.gcd(total, 2048)
+    width = math.gcd(total, 4096)
     return pl.pallas_call(
         attend_kernel,
         out_shape=jax.ShapeDtypeStruct((HD, total), jnp.bfloat16),

time: 160 us -> 153 us (0.956); the launches traced: 163 us -> 151 us
  Pallas kernels: 160 us -> 148 us
    pallas_call x1, Pallas kernels: 34.3 us -> 26.7 us  [attend(): pl.pallas_call(attend_kernel, out_shape=jax.ShapeDtypeStruct((HD, total),...]
    pallas_call x1, Pallas kernels: 83.8 us -> 79.3 us  [encoder_block(): pl.pallas_call(functools.partial(block_kernel, ring, share, sides), out_s...]
where the time goes in v3:
time: 153 us; the launch traced here: 151 us
  Pallas kernels  148 us (97%)
  local copies, waits for them, and re-layouts  2.06 us (1%)
    pallas_call x1, Pallas kernels, encoder_block(): pl.pallas_call(functools.partial(block_kernel, ring, share, sides), out_s...  79.3 us
    pallas_call x1, Pallas kernels, scatter_heads(): pl.pallas_call(functools.partial(scatter_kernel, ring, share, sides), out...  41.8 us
    pallas_call x1, Pallas kernels, attend(): pl.pallas_call(attend_kernel, out_shape=jax.ShapeDtypeStruct((HD, total),...  26.7 us

profile of v3, /device:TPU:0, one launch (start us, length us, event | category | flops | bytes accessed | tf_op | source)
XLA Modules:
  0.0 150.6 jit_solution(15949973832499616550)
XLA Ops:
  0.6 0.0 copy-start.4
  0.6 41.8 %scatter_heads.1 = (bf16[16,64,256]{2,1,0:T(8,128)(2,1)S(1)}, bf16[16,512,128]{2,1,0:T(8,128)(2,1)S(1)}, bf16[2,512,1024]{2,1,0:T(8,128)(2,1)S(1)}, bf16[256,512]{1,0:T(8,128)(2,1)S(1)}) custom-call(bf16[512,1024]{1,0:T(8,128)(2,1)} %tokens_hbm.3, f32[1,1024]{1,0:T(1,128)} %bitcast.20, bf16[3,1024,512]{2,1,0:T(8,128)(2,1)} %qkv_hbm.1, ...), custom_call_target="tpu_custom_call" | custom-call | tf_op jit(solution)/shard_map/scatter_heads/pallas_call | solution.py:236
  42.4 0.0 copy-start.1
  42.5 0.0 copy-start
  42.5 0.0 copy-start.2
  42.5 0.0 copy-start.3
  42.5 0.0 copy-start.5
  42.5 0.0 copy-done.4
  42.6 26.7 %attend.1 = bf16[64,4096]{1,0:T(8,128)(2,1)S(1)} custom-call(s32[16]{0:T(128)S(1)} %copy-done.4, bf16[64,4096]{1,0:T(8,128)(2,1)S(1)} %bitcast.15, bf16[16,512,128]{2,1,0:T(8,128)(2,1)S(1)} %get-tuple-element.7.kv_ref), custom_call_target="tpu_custom_call" | custom-call | tf_op jit(solution)/shard_map/attend/pallas_call | solution.py:780
  69.3 0.0 copy-done.1
  69.3 0.0 copy-done
  69.3 0.0 copy-done.2
  69.3 0.0 copy-done.3
  69.3 0.0 copy-done.5
  69.3 79.3 %encoder_block.1 = (bf16[512,1024]{1,0:T(8,128)(2,1)S(1)}, bf16[512,1024]{1,0:T(8,128)(2,1)S(1)}) custom-call(bf16[16,64,256]{2,1,0:T(8,128)(2,1)S(1)} %bitcast.14, s32[16]{0:T(128)S(1)} %copy-done.4, s32[4]{0:T(128)S(1)} %copy-done.5, bf16[512,1024]{1,0:T(8,128)(2,1)S(1)} %copy-done, f32[1,1024]{1,0:T(1,128)S(1)} %bitcast.18, f32[1,1024]{1,0:T(1,128)S(1)} %bitcast.19, ...), custom_call_target="tpu_custom_call" | custom-call | tf_op jit(solution)/shard_map/encoder_block/pallas_call | solution.py:653
  148.6 1.0 copy.26
  149.6 1.0 copy.27
  (2 shorter events, 0.1 us)
Async XLA Ops:
  0.6 41.9 %copy-start.4 = (s32[16]{0:T(128)S(1)}, s32[16]{0:T(128)}, u32[]{:S(2)}) copy-start(s32[16]{0:T(128)} %pad_lengths.1) | copy-start | bytes 196
  42.4 26.8 %copy-start.1 = (bf16[2,512,1024]{2,1,0:T(8,128)(2,1)}, bf16[2,512,1024]{2,1,0:T(8,128)(2,1)S(1)}, u32[]{:S(2)}) copy-start(bf16[2,512,1024]{2,1,0:T(8,128)(2,1)S(1)} %get-tuple-element.8.w_all_hbm) | copy-start | bytes 6291460
  42.5 26.8 %copy-start = (bf16[512,1024]{1,0:T(8,128)(2,1)S(1)}, bf16[512,1024]{1,0:T(8,128)(2,1)}, u32[]{:S(2)}) copy-start(bf16[512,1024]{1,0:T(8,128)(2,1)} %tokens_hbm.3) | copy-start | bytes 3145732
  42.5 26.8 %copy-start.2 = (f32[1024]{0:T(1024)S(1)}, f32[1024]{0:T(1024)}, u32[]{:S(2)}) copy-start(f32[1024]{0:T(1024)} %param.19) | copy-start | bytes 12292
  42.5 26.8 %copy-start.3 = (f32[1024]{0:T(1024)S(1)}, f32[1024]{0:T(1024)}, u32[]{:S(2)}) copy-start(f32[1024]{0:T(1024)} %param.22) | copy-start | bytes 12292
  42.5 26.8 %copy-start.5 = (s32[4]{0:T(128)S(1)}, s32[4]{0:T(128)}, u32[]{:S(2)}) copy-start(s32[4]{0:T(128)} %target_lengths.1) | copy-start | bytes 52

commit v4 on v3

--- a/solution.py
+++ b/solution.py
@@ -84,9 +84,9 @@
 
 def scatter_kernel(
     ring, share, sides, tokens_hbm, gain_hbm, qkv_hbm, out_hbm, targets_hbm, g_cross_hbm, w_cross_hbm,
-    q_out, kv_out, out_all, cross_q,
+    w_kv_hbm, q_out, kv_out, out_all, w_kv_all, cross_q,
     tokens, gain, qkv, targets, g_cross, w_cross, normed, q_in, kv_in,
-    qs, qr, ks, kr, fs, fr, ls, os, ws, wr,
+    qs, qr, ks, kr, fs, fr, ls, os, ws, wr, vs, vr,
 ):
     me = lax.axis_index("seq")
     here = lax.axis_index("head")
@@ -113,8 +113,28 @@
     for load in loads:
         load.start()
     greet_all(ring, sides)
+    core = lax.rem(me, 2)
+    out_rows = out_hbm.shape[0] // 2
+
+    def out_half(which):
+        return rows_at(which * out_rows, out_rows, out_rows)
+
+    def weight_copy(k, n, side):
+        source = (out_hbm.at[out_half(core)], w_kv_hbm.at[core])[n]
+        target = (out_all.at[side, out_half(core)], w_kv_all.at[side, core])[n]
+        return side_copy(sides, k, source, target, ws.at[k, n], wr.at[k, n])
+
+    def weight_forward(k, n, which):
+        side = lax.rem(here - k + sides, sides)
+        block = (out_all.at[side, out_half(which)], w_kv_all.at[side, which])[n]
+        return seq_copy(flip(me, 1, ring), block, block, vs.at[k, n], vr.at[k, n])
+
+    def query_copy(k, side):
+        return side_copy(sides, k, cross_q.at[here], cross_q.at[side], ws.at[k, 2], wr.at[k, 2])
+
     for k in range(1, sides):
-        side_copy(sides, k, out_hbm, out_all.at[here], ws.at[k], wr.at[k]).start()
+        for n in range(2):
+            weight_copy(k, n, here).start()
 
     def q_copy(i):
         to = flip(me, i, ring)
@@ -189,9 +209,11 @@
     for load in loads[5:]:
         load.wait()
     cross_normed = norm_rows(targets[...].astype(jnp.float32), g_cross[...]).astype(jnp.bfloat16)
-    cross_q[...] = (
+    cross_q[here] = (
         jnp.dot(cross_normed, w_cross[...], preferred_element_type=jnp.float32) * scaling
     ).astype(jnp.bfloat16)
+    for k in range(1, sides):
+        query_copy(k, here).start()
 
     def relay(i, carry):
         origin = flip(me, i, ring)
@@ -218,13 +240,21 @@
         return carry
 
     lax.fori_loop(0, ring, drain, 0)
+    for n in range(2):
+        for k in range(1, sides):
+            weight_copy(k, n, lax.rem(here - k + sides, sides)).wait_recv()
+            weight_forward(k, n, core).start()
     for k in range(1, sides):
-        origin = lax.rem(here - k + sides, sides)
-        side_copy(sides, k, out_hbm, out_all.at[origin], ws.at[k], wr.at[k]).wait()
+        query_copy(k, lax.rem(here - k + sides, sides)).wait_recv()
+        query_copy(k, here).wait_send()
+        for n in range(2):
+            weight_copy(k, n, here).wait_send()
+            weight_forward(k, n, core).wait_send()
+            weight_forward(k, n, 1 - core).wait_recv()
     own_q.wait()
 
 
-def scatter_heads(ring, share, sides, tokens, gain, qkv, w_out, targets, g_cross, w_cross):
+def scatter_heads(ring, share, sides, tokens, gain, qkv, w_out, targets, g_cross, w_cross, w_kv):
     rows, width = tokens.shape
     heads = ring // share
     part = rows // share
@@ -239,10 +269,11 @@
             jax.ShapeDtypeStruct((ring, HD, part), bf16),
             jax.ShapeDtypeStruct((ring, rows, 2 * HD), bf16),
             jax.ShapeDtypeStruct((sides,) + w_out.shape, bf16),
-            jax.ShapeDtypeStruct((half, w_cross.shape[1]), bf16),
+            jax.ShapeDtypeStruct((sides,) + w_kv.shape, bf16),
+            jax.ShapeDtypeStruct((sides, half, w_cross.shape[1]), bf16),
         ),
-        in_specs=[hbm] * 7,
-        out_specs=(vmem, vmem, hbm, vmem),
+        in_specs=[hbm] * 8,
+        out_specs=(vmem, vmem, hbm, hbm, vmem),
         scratch_shapes=[
             pltpu.VMEM((rows, width), bf16),
             pltpu.VMEM((1, width), jnp.float32),
@@ -261,23 +292,25 @@
             dma((ring, share)),
             dma((8,)),
             dma((2,)),
-            dma((sides,)),
-            dma((sides,)),
+            dma((sides, 3)),
+            dma((sides, 3)),
+            dma((sides, 2)),
+            dma((sides, 2)),
         ],
         compiler_params=pltpu.CompilerParams(
             collective_id=0, has_side_effects=True, vmem_limit_bytes=40 * 1024 * 1024
         ),
         name="scatter_heads",
-    )(*map(in_hbm, (tokens, gain[None, :], qkv, w_out, targets, g_cross[None, :], w_cross)))
+    )(*map(in_hbm, (tokens, gain[None, :], qkv, w_out, targets, g_cross[None, :], w_cross, w_kv)))
 
 
 def block_kernel(
     ring, share, sides, x_in, pad_lengths, target_lengths, tokens_hbm, g_ffn_hbm, g_final_hbm,
-    w_own_hbm, w_all_hbm, up_hbm, down_hbm, kv_hbm, cross_q, w_cross_hbm, targets_hbm,
+    w_own_hbm, w_all_hbm, up_hbm, down_hbm, kv_hbm, kv_all_hbm, cross_q, w_cross_hbm, targets_hbm,
     encoded, decoded,
-    tokens, g_ffn, g_final, w_out, context, hidden, normed, parts, up, down, w_kv, w_cross, mine,
-    cross_k, cross_v, mixed, stats, got, partial, incoming,
-    ls, ss, rs, fs, fr, ps, pr, cs, cr, ms, mr, xs, xr, zs, zr, ws, wr, hs, hr,
+    tokens, g_ffn, g_final, w_out, context, hidden, normed, parts, landed, up, down, w_kv, w_cross,
+    mine, cross_k, cross_v, given, taken, mixed, stats, got, partial, incoming,
+    ls, ss, rs, fs, fr, ps, pr, cs, cr, es, er, ts, tr, ms, mr, xs, xr, zs, zr, ws, wr, hs, hr,
 ):
     me = lax.axis_index("seq")
     here = lax.axis_index("head")
@@ -300,7 +333,7 @@
                 (up_hbm, up),
                 (down_hbm, down),
                 (g_final_hbm, g_final),
-                (kv_hbm, w_kv),
+                (kv_hbm, w_kv.at[here]),
                 (w_cross_hbm, w_cross),
                 (targets_hbm.at[rows_at(slab_start(me), slab, slab)], mine),
             ]
@@ -308,6 +341,10 @@
                 (w_all_hbm.at[lax.rem(here + k, sides)], w_out.at[lax.rem(here + k, sides)])
                 for k in range(1, sides)
             ]
+            + [
+                (kv_all_hbm.at[lax.rem(here + k, sides)], w_kv.at[lax.rem(here + k, sides)])
+                for k in range(1, sides)
+            ]
         )
     ]
     for load in loads:
@@ -360,7 +397,7 @@
         return carry
 
     lax.fori_loop(0, ring, drain, 0)
-    for load in loads[:3] + loads[9:]:
+    for load in loads[:3] + loads[9 : 8 + sides]:
         load.wait()
     part = rows // share
 
@@ -378,54 +415,65 @@
     lax.fori_loop(0, share, project, 0)
     for load in loads[3:6]:
         load.wait()
-    chunk = math.gcd(rows, 128)
-    chunks = rows // chunk
+    lot = rows // sides
+    chunk = math.gcd(lot, 128)
+    chunks = lot // chunk
 
     def span(c):
         return rows_at(c * chunk, chunk, chunk)
 
-    def swap(c, k, side):
+    def hand_over(c, k, side, origin):
         return side_copy(
-            sides, k, parts.at[side, span(c)], parts.at[side, span(c)], ps.at[c, k], pr.at[c, k]
-        )
-
-    def feed(c, carry):
-        x = normed[span(c), :]
+            sides, k, parts.at[side, span(c)], landed.at[origin, span(c)], ps.at[c, k], pr.at[c, k]
+        )
+
+    def feed(n, carry):
+        k = lax.div(n, chunks) + 1
+        c = lax.rem(n, chunks)
+        side = lax.rem(here + k, sides)
+        x = normed[rows_at(side * lot + c * chunk, chunk, chunk), :]
         gate = jnp.dot(x, up[0], preferred_element_type=jnp.float32)
         lift = jnp.dot(x, up[1], preferred_element_type=jnp.float32)
         active = (jax.nn.gelu(gate, approximate=True) * lift).astype(jnp.bfloat16)
-        parts[here, span(c), :] = jnp.dot(
+        parts[side, span(c), :] = jnp.dot(
             active, down[...], preferred_element_type=jnp.float32
         ).astype(jnp.bfloat16)
+
+        @pl.when(k < sides)
+        def away():
+            hand_over(c, k, side, here).start()
+
+        return carry
+
+    lax.fori_loop(0, sides * chunks, feed, 0)
+    for load in loads[6:9] + loads[8 + sides :]:
+        load.wait()
+
+    def pair_up(c, slot):
+        return [
+            seq_copy(
+                mate, whole.at[slot, side, span(c)], whole.at[slot, side, span(c)],
+                cs.at[c, side, n], cr.at[c, side, n],
+            )
+            for n, whole in enumerate((cross_k, cross_v))
+            for side in range(sides)
+        ]
+
+    def close(c, carry):
+        at = rows_at(here * lot + c * chunk, chunk, chunk)
+        total = hidden[at, :] + parts[here, span(c), :].astype(jnp.float32)
         for k in range(1, sides):
-            swap(c, k, here).start()
-        return carry
-
-    lax.fori_loop(0, chunks, feed, 0)
-    for load in loads[6:9]:
-        load.wait()
-
-    def pair_up(c, slot):
-        return (
-            seq_copy(mate, cross_k.at[slot, span(c)], cross_k.at[slot, span(c)], cs.at[c, 0], cr.at[c, 0]),
-            seq_copy(mate, cross_v.at[slot, span(c)], cross_v.at[slot, span(c)], cs.at[c, 1], cr.at[c, 1]),
-        )
-
-    def close(c, carry):
-        for k in range(1, sides):
-            swap(c, k, here).wait_send()
-            swap(c, k, lax.rem(here - k + sides, sides)).wait_recv()
-        total = hidden[span(c), :]
-        for side in range(sides):
-            total = total + parts[side, span(c), :].astype(jnp.float32)
+            origin = lax.rem(here - k + sides, sides)
+            hand_over(c, k, lax.rem(here + k, sides), here).wait_send()
+            hand_over(c, k, here, origin).wait_recv()
+            total = total + landed[origin, span(c), :].astype(jnp.float32)
         done = norm_rows(total, g_final[...]).astype(jnp.bfloat16)
-        encoded[span(c), :] = done
-        cross_k[core, span(c), :] = jnp.dot(
-            done, w_kv[0], preferred_element_type=jnp.float32
-        ).astype(jnp.bfloat16)
-        cross_v[core, span(c), :] = jnp.dot(
-            done, w_kv[1], preferred_element_type=jnp.float32
-        ).astype(jnp.bfloat16)
+        encoded[at, :] = done
+        for n, whole in enumerate((cross_k, cross_v)):
+            for side in range(sides):
+                whole[core, side, span(c), :] = jnp.dot(
+                    done, w_kv[side, n], preferred_element_type=jnp.float32
+                ).astype(jnp.bfloat16)
         for copy in pair_up(c, core):
             copy.start()
         return carry
@@ -440,17 +488,104 @@
         return carry
 
     lax.fori_loop(0, chunks, paired, 0)
-    half = cross_q.shape[0]
+    half = cross_q.shape[1]
     pairs = heads // 2
     peers = ring // 2
-    position = lax.broadcasted_iota(jnp.int32, (2 * rows, 2 * HD), 0)
+    position = lax.broadcasted_iota(jnp.int32, (2 * lot, 2 * HD), 0)
     first = me - core
-    limit = jnp.where(position < rows, pad_lengths[first], rows + pad_lengths[first + 1])
+    limit = jnp.where(position < lot, pad_lengths[first], lot + pad_lengths[first + 1]) - here * lot
     dead = jnp.where(position < limit, 0.0, masked_score).astype(jnp.bfloat16)
-    lane = lax.broadcasted_iota(jnp.int32, (2 * rows, 2 * HD), 1)
+    lane = lax.broadcasted_iota(jnp.int32, (2 * lot, 2 * HD), 1)
     out_lane = lax.broadcasted_iota(jnp.int32, (half, 2 * HD), 1)
-    ones = jnp.ones((2 * rows, 2 * HD), jnp.bfloat16)
-    stats[...] = jnp.where(out_lane < HD, 0.0, jnp.where(out_lane < HD + heads, 1.0, 0.0))
+    ones = jnp.ones((2 * lot, 2 * HD), jnp.bfloat16)
+
+    def pack(seen):
+        high = seen.astype(jnp.bfloat16).astype(jnp.float32)
+        rest = seen - high
+        middle = rest.astype(jnp.bfloat16).astype(jnp.float32)
+        return (
+            high + pltpu.roll(middle, heads, 1) + pltpu.roll(rest - middle, 2 * heads, 1)
+        ).astype(jnp.bfloat16)
+
+    def unpack(packed):
+        return (
+            packed
+            + pltpu.roll(packed, 2 * HD - heads, 1)
+            + pltpu.roll(packed, 2 * HD - 2 * heads, 1)
+        )
+
+    def to_owner(k, i, side, origin):
+        return side_copy(sides, k, given.at[side, i], taken.at[origin, i], ts.at[k, i], tr.at[k, i])
+
+    def attend_side(k, carry):
+        side = lax.rem(here + k, sides)
+        stats[...] = jnp.where(out_lane < HD, 0.0, jnp.where(out_lane < HD + heads, 1.0, 0.0))
+
+        def cross_pair(i, carry):
+            cut = rows_at(i * 2 * HD, 2 * HD, 2 * HD)
+            q_here = cross_q[side, :, cut]
+            k_here = cross_k[:, side, :, cut].reshape(2 * lot, 2 * HD)
+            v_here = cross_v[:, side, :, cut].reshape(2 * lot, 2 * HD)
+            pieces = []
+            seen = stats[...]
+            for h in range(2):
+                own = lane < HD if h == 0 else lane >= HD
+                keys = jnp.where(own, k_here, dead)
+                values = jnp.where(own, v_here, ones)
+                pick = jnp.where(out_lane == (HD if h == 0 else 0), 1.0, 0.0).astype(jnp.bfloat16)
+                queries = jnp.where(out_lane < HD if h == 0 else out_lane >= HD, q_here, pick)
+                scores = lax.dot_general(
+                    queries, keys, (((1,), (1,)), ((), ())), preferred_element_type=jnp.float32
+                )
+                top = jnp.max(scores, axis=1, keepdims=True)
+                weights = jnp.exp2(scores - top).astype(jnp.bfloat16)
+                piece = jnp.dot(weights, values, preferred_element_type=jnp.float32)
+                total = piece[:, 2 * HD - 1 :] if h == 0 else piece[:, :1]
+                seen = jnp.where(
+                    out_lane == 2 * i + h, top, jnp.where(out_lane == HD + 2 * i + h, total, seen)
+                )
+                pieces.append(piece)
+            stats[...] = seen
+            given[side, i] = jnp.where(out_lane < HD, pieces[0], pieces[1]).astype(jnp.bfloat16)
+
+            @pl.when(k < sides)
+            def away():
+                to_owner(k, i, side, here).start()
+
+            return carry
+
+        lax.fori_loop(0, pairs, cross_pair, 0)
+
+        @pl.when(k < sides)
+        def summary():
+            given[side, pairs] = pack(stats[...])
+            to_owner(k, pairs, side, here).start()
+
+        return carry
+
+    lax.fori_loop(1, sides + 1, attend_side, 0)
+
+    def publish(k, side):
+        rows_of = encoded.at[rows_at(side * lot, lot, lot)]
+        return side_copy(sides, k, rows_of, rows_of, es.at[k], er.at[k])
+
+    for k in range(1, sides):
+        publish(k, here).start()
+    for k in range(1, sides):
+        for i in range(pairs + 1):
+            to_owner(k, i, here, lax.rem(here - k + sides, sides)).wait_recv()
+    origins = [lax.rem(here - k + sides, sides) for k in range(1, sides)]
+    views = [stats[...]] + [unpack(taken[o, pairs].astype(jnp.float32)) for o in origins]
+    best = functools.reduce(jnp.maximum, views)
+    grows = [jnp.where(out_lane < heads, jnp.exp2(view - best), 0.0) for view in views]
+    weight_sum = sum(grow * pltpu.roll(view, HD, 1) for grow, view in zip(grows, views))
+    column = lax.broadcasted_iota(jnp.int32, (2 * HD, heads * HD), 1)
+    row = lax.broadcasted_iota(jnp.int32, (2 * HD, heads * HD), 0)
+    spread = jnp.where((column >= row * HD) & (column < row * HD + HD), 1.0, 0.0)
+    scales = jnp.dot(
+        jnp.concatenate(grows, axis=0), spread, precision=lax.Precision.HIGHEST,
+        preferred_element_type=jnp.float32,
+    )
 
     def to_peer(i, j):
         to = flip(me, 2 * j, ring)
@@ -464,43 +599,23 @@
 
         lax.fori_loop(1, peers, send_one, 0)
 
-    def cross_pair(i, carry):
-        cut = rows_at(i * 2 * HD, 2 * HD, 2 * HD)
-        q_here = cross_q[:, cut]
-        k_here = cross_k[:, :, cut].reshape(2 * rows, 2 * HD)
-        v_here = cross_v[:, :, cut].reshape(2 * rows, 2 * HD)
-        pieces = []
-        seen = stats[...]
-        for h in range(2):
-            own = lane < HD if h == 0 else lane >= HD
-            keys = jnp.where(own, k_here, dead)
-            values = jnp.where(own, v_here, ones)
-            pick = jnp.where(out_lane == (HD if h == 0 else 0), 1.0, 0.0).astype(jnp.bfloat16)
-            queries = jnp.where(out_lane < HD if h == 0 else out_lane >= HD, q_here, pick)
-            scores = lax.dot_general(
-                queries, keys, (((1,), (1,)), ((), ())), preferred_element_type=jnp.float32
-            )
-            top = jnp.max(scores, axis=1, keepdims=True)
-            weights = jnp.exp2(scores - top).astype(jnp.bfloat16)
-            piece = jnp.dot(weights, values, preferred_element_type=jnp.float32)
-            total = piece[:, 2 * HD - 1 :] if h == 0 else piece[:, :1]
-            seen = jnp.where(
-                out_lane == 2 * i + h, top, jnp.where(out_lane == HD + 2 * i + h, total, seen)
-            )
-            pieces.append(piece)
-        stats[...] = seen
-        mixed[i] = jnp.where(out_lane < HD, pieces[0], pieces[1]).astype(jnp.bfloat16)
+    for i in range(pairs):
+        cut = slice(i * 2 * HD, (i + 1) * 2 * HD)
+        total = given[here, i].astype(jnp.float32) * scales[:half, cut]
+        for n, origin in enumerate(origins):
+            scale = scales[(n + 1) * half : (n + 2) * half, cut]
+            total = total + taken[origin, i].astype(jnp.float32) * scale
+        mixed[i] = total.astype(jnp.bfloat16)
         to_peers(i)
-        return carry
-
-    lax.fori_loop(0, pairs, cross_pair, 0)
-    seen = stats[...]
-    high = seen.astype(jnp.bfloat16).astype(jnp.float32)
-    rest = seen - high
-    middle = rest.astype(jnp.bfloat16).astype(jnp.float32)
-    mixed[pairs] = (
-        high + pltpu.roll(middle, heads, 1) + pltpu.roll(rest - middle, 2 * heads, 1)
-    ).astype(jnp.bfloat16)
+    mixed[pairs] = pack(
+        jnp.where(
+            out_lane < heads,
+            best,
+            jnp.where(
+                (out_lane >= HD) & (out_lane < HD + heads), pltpu.roll(weight_sum, HD, 1), 0.0
+            ),
+        )
+    )
     to_peers(pairs)
     got[0] = mixed[:, rows_at(lax.div(me, 2) * slab, slab, slab), :]
 
@@ -512,8 +627,7 @@
         return carry
 
     lax.fori_loop(1, peers, collect, 0)
-    packed = got[:, pairs].astype(jnp.float32).reshape(peers * slab, 2 * HD)
-    seen = packed + pltpu.roll(packed, 2 * HD - heads, 1) + pltpu.roll(packed, 2 * HD - 2 * heads, 1)
+    seen = unpack(got[:, pairs].astype(jnp.float32).reshape(peers * slab, 2 * HD))
     sums = pltpu.roll(seen, HD, 1).reshape(peers, slab, 2 * HD)
     seen = seen.reshape(peers, slab, 2 * HD)
     best = jnp.max(seen, axis=0, keepdims=True)
@@ -521,9 +635,6 @@
     weight_sum = jnp.sum(grow * sums, axis=0, keepdims=True)
     factor = (grow / weight_sum).reshape(peers * slab, 2 * HD)
     factor = jnp.where(lax.broadcasted_iota(jnp.int32, factor.shape, 1) < heads, factor, 0.0)
-    column = lax.broadcasted_iota(jnp.int32, (2 * HD, heads * HD), 1)
-    row = lax.broadcasted_iota(jnp.int32, (2 * HD, heads * HD), 0)
-    spread = jnp.where((column >= row * HD) & (column < row * HD + HD), 1.0, 0.0)
     wide = jnp.dot(
         factor, spread, precision=lax.Precision.HIGHEST, preferred_element_type=jnp.float32
     ).reshape(peers, slab, heads * HD)
@@ -587,7 +698,7 @@
         source = block(flip(owner, 2 * n, ring), side)
         return seq_copy(mate, source, source, hs.at[k, n], hr.at[k, n])
 
-    given = range(1, sides) if divided else ()
+    beside = range(1, sides) if divided else ()
 
     def share_out(n, carry):
         to_near(n, me).start()
@@ -596,7 +707,7 @@
     lax.fori_loop(1, peers, share_out, 0)
 
     def pass_block(n):
-        for k in given:
+        for k in beside:
             to_side(k, n, here).start()
         to_mate(0, n, me).start()
 
@@ -610,7 +721,7 @@
     lax.fori_loop(1, peers, pass_along, 0)
 
     def across(n, carry):
-        for k in given:
+        for k in beside:
             to_side(k, n, lax.rem(here - k + sides, sides)).wait_recv()
             to_mate(k, n, me).start()
         return carry
@@ -623,26 +734,32 @@
     lax.fori_loop(1, peers, spent, 0)
 
     def settle(n, carry):
-        for k in given:
+        for k in beside:
             to_side(k, n, here).wait_send()
-        for k in (0, *given):
+        for k in (0, *beside):
             to_mate(k, n, me).wait_send()
             to_mate(k, n, mate).wait_recv()
         return carry
 
     lax.fori_loop(0, peers, settle, 0)
+    for k in range(1, sides):
+        publish(k, here).wait_send()
+        publish(k, lax.rem(here - k + sides, sides)).wait_recv()
+        for i in range(pairs + 1):
+            to_owner(k, i, lax.rem(here + k, sides), here).wait_send()
 
 
 def encoder_block(
     ring, share, sides, back, pad_lengths, target_lengths, tokens, g_ffn, g_final, w_own, w_all,
-    ffn_in, ffn_out, w_kv, cross_q, w_cross, targets,
+    ffn_in, ffn_out, w_kv, w_kv_all, cross_q, w_cross, targets,
 ):
     rows, width = tokens.shape
     heads = ring // share
-    chunks = rows // math.gcd(rows, 128)
+    lot = rows // sides
+    chunks = lot // math.gcd(lot, 128)
     slab = targets.shape[0] // ring
     piece = slab // sides if slab % (16 * sides) == 0 else slab
-    half, lanes = cross_q.shape
+    half, lanes = cross_q.shape[1:]
     pairs = heads // 2
     peers = ring // 2
     bf16 = jnp.bfloat16
@@ -656,7 +773,7 @@
             jax.ShapeDtypeStruct((rows, width), bf16),
             jax.ShapeDtypeStruct(targets.shape, bf16),
         ),
-        in_specs=[vmem, smem, smem] + [hbm] * 8 + [vmem, hbm, hbm],
+        in_specs=[vmem, smem, smem] + [hbm] * 9 + [vmem, hbm, hbm],
         out_specs=(vmem, vmem),
         scratch_shapes=[
             pltpu.VMEM((rows, width), bf16),
@@ -666,28 +783,35 @@
             pltpu.VMEM((share, sides * heads, HD, rows // share), bf16),
             pltpu.VMEM((rows, width), jnp.float32),
             pltpu.VMEM((rows, width), bf16),
-            pltpu.VMEM((sides, rows, width), bf16),
+            pltpu.VMEM((sides, lot, width), bf16),
+            pltpu.VMEM((sides, lot, width), bf16),
             pltpu.VMEM(ffn_in.shape, bf16),
             pltpu.VMEM(ffn_out.shape, bf16),
-            pltpu.VMEM(w_kv.shape, bf16),
+            pltpu.VMEM((sides,) + w_kv.shape, bf16),
             pltpu.VMEM(w_cross.shape, bf16),
             pltpu.VMEM((slab, width), bf16),
-            pltpu.VMEM((2, rows, lanes), bf16),
-            pltpu.VMEM((2, rows, lanes), bf16),
+            pltpu.VMEM((2, sides, lot, lanes), bf16),
+            pltpu.VMEM((2, sides, lot, lanes), bf16),
+            pltpu.VMEM((sides, pairs + 1, half, 2 * HD), bf16),
+            pltpu.VMEM((sides, pairs + 1, half, 2 * HD), bf16),
             pltpu.VMEM((pairs + 1, half, 2 * HD), bf16),
             pltpu.VMEM((half, 2 * HD), jnp.float32),
             pltpu.VMEM((peers, pairs + 1, slab, 2 * HD), bf16),
             pltpu.VMEM((slab, width), bf16),
             pltpu.VMEM((sides, piece, width), bf16),
-            dma((9 + sides,)),
+            dma((8 + 2 * sides,)),
             dma((ring,)),
             dma((ring,)),
             dma((ring, sides)),
             dma((ring, sides)),
             dma((chunks, sides)),
             dma((chunks, sides)),
-            dma((chunks, 2)),
-            dma((chunks, 2)),
+            dma((chunks, sides, 2)),
+            dma((chunks, sides, 2)),
+            dma((sides,)),
+            dma((sides,)),
+            dma((sides, pairs + 1)),
+            dma((sides, pairs + 1)),
             dma((peers, pairs + 1)),
             dma((peers, pairs + 1)),
             dma((sides,)),
@@ -705,7 +829,7 @@
         name="encoder_block",
     )(
         back, pad_lengths, target_lengths, tokens, g_ffn[None, :], g_final[None, :], w_own, w_all,
-        ffn_in, ffn_out, w_kv, cross_q, w_cross, targets,
+        ffn_in, ffn_out, w_kv, w_kv_all, cross_q, w_cross, targets,
     )
 
 
@@ -824,8 +948,9 @@
     heads_here = self_qkv.shape[2] // HD
     share = ring // heads_here
     part = tokens.shape[0] // share
-    q_got, kv_got, out_all, cross_q = scatter_heads(
-        ring, share, sides, tokens, norm_attn, self_qkv, self_out, targets, norm_cross, cross_query
+    q_got, kv_got, out_all, cross_kv_all, cross_q = scatter_heads(
+        ring, share, sides, tokens, norm_attn, self_qkv, self_out, targets, norm_cross, cross_query,
+        cross_kv,
     )
     q_all = q_got.transpose(1, 0, 2).reshape(HD, ring * part)
     mixed_t = attend(q_all, kv_got, pad_lengths)
@@ -845,6 +970,7 @@
         ffn_in,
         ffn_out,
         cross_kv,
+        cross_kv_all,
         cross_q,
         cross_out,
         targets,

time: 153 us -> 157 us (1.026)
  Pallas kernels: 148 us -> 151 us
  local copies, waits for them, and re-layouts: 2.06 us -> 3.97 us
    pallas_call x1, Pallas kernels: 41.8 us -> 49.5 us  [scatter_heads(): pl.pallas_call(functools.partial(scatter_kernel, ring, share, sides), out...]
    pallas_call x1, Pallas kernels: 79.3 us -> 74.4 us  [encoder_block(): pl.pallas_call(functools.partial(block_kernel, ring, share, sides), out_s...]
    unnamed x14, local copies, waits for them, and re-layouts: 1.98 us -> 3.89 us
where the time goes in v4:
time: 157 us; the launch traced here: 155 us
  Pallas kernels  151 us (96%)
  local copies, waits for them, and re-layouts  3.97 us (3%)
    pallas_call x1, Pallas kernels, encoder_block(): pl.pallas_call(functools.partial(block_kernel, ring, share, sides), out_s...  74.4 us
    pallas_call x1, Pallas kernels, scatter_heads(): pl.pallas_call(functools.partial(scatter_kernel, ring, share, sides), out...  49.5 us
    pallas_call x1, Pallas kernels, attend(): pl.pallas_call(attend_kernel, out_shape=jax.ShapeDtypeStruct((HD, total),...  26.8 us
    unnamed x14, local copies, waits for them, and re-layouts  3.89 us

profile of v4, /device:TPU:0, one launch (start us, length us, event | category | flops | bytes accessed | tf_op | source)
XLA Modules:
  0.0 155.4 jit_solution(7305989088756561607)
XLA Ops:
  0.6 0.0 copy-start.4
  0.6 49.5 %scatter_heads.1 = (bf16[16,64,256]{2,1,0:T(8,128)(2,1)S(1)}, bf16[16,512,128]{2,1,0:T(8,128)(2,1)S(1)}, bf16[2,512,1024]{2,1,0:T(8,128)(2,1)S(1)}, bf16[2,2,102...) custom-call(bf16[512,1024]{1,0:T(8,128)(2,1)} %tokens_hbm.3, f32[1,1024]{1,0:T(1,128)} %bitcast.20, ...), custom_call_target="tpu_custom_call" | custom-call | tf_op jit(solution)/shard_map/scatter_heads/pallas_call | solution.py:266
  50.2 0.0 copy-start
  50.2 1.9 %copy-done = bf16[2,2,1024,512]{3,2,1,0:T(8,128)(2,1)} copy-done((bf16[2,2,1024,512]{3,2,1,0:T(8,128)(2,1)}, bf16[2,2,1024,512]{3,2,1,0:T(8,128)(2,1)S(1)}, u32[]{:S(2)}) %copy-start) | copy-done | bytes 4194328
  52.1 0.0 copy-start.1
  52.1 0.0 copy-start.2
  52.1 0.0 copy-start.3
  52.1 0.0 copy-start.5
  52.2 0.0 copy-done.4
  52.2 26.8 %attend.1 = bf16[64,4096]{1,0:T(8,128)(2,1)S(1)} custom-call(s32[16]{0:T(128)S(1)} %copy-done.4, bf16[64,4096]{1,0:T(8,128)(2,1)S(1)} %bitcast.14, bf16[16,512,128]{2,1,0:T(8,128)(2,1)S(1)} %get-tuple-element.8.kv_ref), custom_call_target="tpu_custom_call" | custom-call | tf_op jit(solution)/shard_map/attend/pallas_call | solution.py:904
  79.1 0.0 copy-done.1
  79.1 0.0 copy-done.2
  79.1 0.0 copy-done.3
  79.1 0.0 copy-done.5
  79.1 74.4 %encoder_block.1 = (bf16[512,1024]{1,0:T(8,128)(2,1)S(1)}, bf16[512,1024]{1,0:T(8,128)(2,1)S(1)}) custom-call(bf16[16,64,256]{2,1,0:T(8,128)(2,1)S(1)} %bitcast.16, s32[16]{0:T(128)S(1)} %copy-done.4, s32[4]{0:T(128)S(1)} %copy-done.5, bf16[512,1024]{1,0:T(8,128)(2,1)} %tokens_hbm.3, f32[1,1024]{1,0:T(1,128)S(1)} %bitcast.18, f32[1,1024]{1,0:T(1,128)S(1)} %bitcast.19, ...), custom_call_target="tpu_custom_call" | custom-call | tf_op jit(solution)/shard_map/encoder_block/pallas_call | solution.py:770
  153.5 1.0 copy.26
  154.5 1.0 copy.27
  (2 shorter events, 0.1 us)
Async XLA Ops:
  0.6 51.5 %copy-start.4 = (s32[16]{0:T(128)S(1)}, s32[16]{0:T(128)}, u32[]{:S(2)}) copy-start(s32[16]{0:T(128)} %pad_lengths.1) | copy-start | bytes 196
  50.2 1.9 %copy-start = (bf16[2,2,1024,512]{3,2,1,0:T(8,128)(2,1)}, bf16[2,2,1024,512]{3,2,1,0:T(8,128)(2,1)S(1)}, u32[]{:S(2)}) copy-start(bf16[2,2,1024,512]{3,2,1,0:T(8,128)(2,1)S(1)} %get-tuple-element.10.kv_all_hbm) | copy-start | bytes 12582916
  52.1 27.0 %copy-start.1 = (bf16[2,512,1024]{2,1,0:T(8,128)(2,1)}, bf16[2,512,1024]{2,1,0:T(8,128)(2,1)S(1)}, u32[]{:S(2)}) copy-start(bf16[2,512,1024]{2,1,0:T(8,128)(2,1)S(1)} %get-tuple-element.9.w_all_hbm) | copy-start | bytes 6291460
  52.1 27.0 %copy-start.2 = (f32[1024]{0:T(1024)S(1)}, f32[1024]{0:T(1024)}, u32[]{:S(2)}) copy-start(f32[1024]{0:T(1024)} %param.19) | copy-start | bytes 12292
  52.1 27.0 %copy-start.3 = (f32[1024]{0:T(1024)S(1)}, f32[1024]{0:T(1024)}, u32[]{:S(2)}) copy-start(f32[1024]{0:T(1024)} %param.22) | copy-start | bytes 12292
  52.1 27.0 %copy-start.5 = (s32[4]{0:T(128)S(1)}, s32[4]{0:T(128)}, u32[]{:S(2)}) copy-start(s32[4]{0:T(128)} %target_lengths.1) | copy-start | bytes 52

commit v5 on v3

--- a/solution.py
+++ b/solution.py
@@ -276,7 +276,7 @@
     w_own_hbm, w_all_hbm, up_hbm, down_hbm, kv_hbm, cross_q, w_cross_hbm, targets_hbm,
     encoded, decoded,
     tokens, g_ffn, g_final, w_out, context, hidden, normed, parts, up, down, w_kv, w_cross, mine,
-    cross_k, cross_v, mixed, stats, got, partial, incoming,
+    cross_k, cross_v, held, tops, mixed, stats, got, partial, incoming,
     ls, ss, rs, fs, fr, ps, pr, cs, cr, ms, mr, xs, xr, zs, zr, ws, wr, hs, hr,
 ):
     me = lax.axis_index("seq")
@@ -464,30 +464,39 @@
 
         lax.fori_loop(1, peers, send_one, 0)
 
+    def score(i, h):
+        cut = rows_at(i * 2 * HD, 2 * HD, 2 * HD)
+        keys = cross_k[:, :, cut].reshape(2 * rows, 2 * HD)
+        keys = jnp.where(lane < HD if h == 0 else lane >= HD, keys, dead)
+        pick = jnp.where(out_lane == (HD if h == 0 else 0), 1.0, 0.0).astype(jnp.bfloat16)
+        queries = jnp.where(out_lane < HD if h == 0 else out_lane >= HD, cross_q[:, cut], pick)
+        return lax.dot_general(
+            queries, keys, (((1,), (1,)), ((), ())), preferred_element_type=jnp.float32
+        )
+
+    def hold(h, scores):
+        held[h] = scores
+        tops[h] = jnp.max(scores, axis=1, keepdims=True)
+
+    for h in range(2):
+        hold(h, score(0, h))
+
     def cross_pair(i, carry):
-        cut = rows_at(i * 2 * HD, 2 * HD, 2 * HD)
-        q_here = cross_q[:, cut]
-        k_here = cross_k[:, :, cut].reshape(2 * rows, 2 * HD)
-        v_here = cross_v[:, :, cut].reshape(2 * rows, 2 * HD)
+        following = [score(lax.rem(i + 1, pairs), h) for h in range(2)]
+        v_here = cross_v[:, :, rows_at(i * 2 * HD, 2 * HD, 2 * HD)].reshape(2 * rows, 2 * HD)
         pieces = []
         seen = stats[...]
         for h in range(2):
-            own = lane < HD if h == 0 else lane >= HD
-            keys = jnp.where(own, k_here, dead)
-            values = jnp.where(own, v_here, ones)
-            pick = jnp.where(out_lane == (HD if h == 0 else 0), 1.0, 0.0).astype(jnp.bfloat16)
-            queries = jnp.where(out_lane < HD if h == 0 else out_lane >= HD, q_here, pick)
-            scores = lax.dot_general(
-                queries, keys, (((1,), (1,)), ((), ())), preferred_element_type=jnp.float32
-            )
-            top = jnp.max(scores, axis=1, keepdims=True)
-            weights = jnp.exp2(scores - top).astype(jnp.bfloat16)
+            values = jnp.where(lane < HD if h == 0 else lane >= HD, v_here, ones)
+            top = tops[h]
+            weights = jnp.exp2(held[h] - top).astype(jnp.bfloat16)
             piece = jnp.dot(weights, values, preferred_element_type=jnp.float32)
             total = piece[:, 2 * HD - 1 :] if h == 0 else piece[:, :1]
             seen = jnp.where(
                 out_lane == 2 * i + h, top, jnp.where(out_lane == HD + 2 * i + h, total, seen)
             )
             pieces.append(piece)
+            hold(h, following[h])
         stats[...] = seen
         mixed[i] = jnp.where(out_lane < HD, pieces[0], pieces[1]).astype(jnp.bfloat16)
         to_peers(i)
@@ -524,8 +533,12 @@
     column = lax.broadcasted_iota(jnp.int32, (2 * HD, heads * HD), 1)
     row = lax.broadcasted_iota(jnp.int32, (2 * HD, heads * HD), 0)
     spread = jnp.where((column >= row * HD) & (column < row * HD + HD), 1.0, 0.0)
+    spread = spread.astype(jnp.bfloat16)
+    high = factor.astype(jnp.bfloat16)
+    low = (factor - high.astype(jnp.float32)).astype(jnp.bfloat16)
     wide = jnp.dot(
-        factor, spread, precision=lax.Precision.HIGHEST, preferred_element_type=jnp.float32
+        jnp.concatenate([high, low], axis=1), jnp.concatenate([spread, spread], axis=0),
+        preferred_element_type=jnp.float32,
     ).reshape(peers, slab, heads * HD)
     merged = []
     for i in range(pairs):
@@ -674,6 +687,8 @@
             pltpu.VMEM((slab, width), bf16),
             pltpu.VMEM((2, rows, lanes), bf16),
             pltpu.VMEM((2, rows, lanes), bf16),
+            pltpu.VMEM((2, half, 2 * rows), jnp.float32),
+            pltpu.VMEM((2, half, 1), jnp.float32),
             pltpu.VMEM((pairs + 1, half, 2 * HD), bf16),
             pltpu.VMEM((half, 2 * HD), jnp.float32),
             pltpu.VMEM((peers, pairs + 1, slab, 2 * HD), bf16),
@@ -709,7 +724,9 @@
     )
 
 
-def attend_kernel(lengths, q_ref, kv_ref, o_ref, keys, values, flipped, count):
+def attend_kernel(
+    lengths, q_ref, kv_ref, o_ref, keys, values, flipped, count, held, tops, reach, mixed
+):
     blocks, span, lanes = kv_ref.shape
     tile = span
     queries = q_ref.shape[1]
@@ -746,37 +763,43 @@
     q_wide = jnp.concatenate([q_ref[...], pick], axis=0)
     cuts = [slice(g, g + group) for g in range(0, queries, group)]
 
-    def step(t, state):
+    def score(t, cut):
         at = pl.ds(pl.multiple_of(t * tile, tile), tile)
-        keys_here = keys[at, :]
+        return jnp.dot(keys[at, :], q_wide[:, cut], preferred_element_type=jnp.float32)
+
+    def hold(n, scores):
+        held[n] = scores
+        tops[n] = jnp.max(scores, axis=0, keepdims=True)
+
+    for n, cut in enumerate(cuts):
+        hold(n, score(0, cut))
+        reach[n] = jnp.full((1, group), masked_score, jnp.float32)
+        mixed[n] = jnp.zeros((ones_rows + HD, group), jnp.float32)
+
+    def step(t, carry):
         values_here = flipped[t]
-        all_scores = [
-            jnp.dot(keys_here, q_wide[:, cut], preferred_element_type=jnp.float32) for cut in cuts
-        ]
-        updated = []
-        for scores, (top, mixed) in zip(all_scores, state):
-            new_top = jnp.maximum(top, jnp.max(scores, axis=0, keepdims=True))
-            weights = jnp.exp2(scores - new_top).astype(jnp.bfloat16)
-            part = jnp.dot(values_here, weights, preferred_element_type=jnp.float32)
-            updated.append((new_top, mixed * jnp.exp2(top - new_top) + part))
-        return tuple(updated)
-
-    start = tuple(
-        (
-            jnp.full((1, group), masked_score, jnp.float32),
-            jnp.zeros((ones_rows + HD, group), jnp.float32),
-        )
-        for cut in cuts
-    )
-    ends = lax.fori_loop(0, count[0], step, start)
-    for cut, (top, mixed) in zip(cuts, ends):
-        o_ref[:, cut] = (mixed[ones_rows:, :] / mixed[0:1, :]).astype(jnp.bfloat16)
+        for n, cut in enumerate(cuts):
+            following = score(t + 1, cut)
+            top = jnp.maximum(reach[n], tops[n])
+            weights = jnp.exp2(held[n] - top).astype(jnp.bfloat16)
+            mixed[n] = mixed[n] * jnp.exp2(reach[n] - top) + jnp.dot(
+                values_here, weights, preferred_element_type=jnp.float32
+            )
+            reach[n] = top
+            hold(n, following)
+        return carry
+
+    lax.fori_loop(0, count[0], step, 0)
+    for n, cut in enumerate(cuts):
+        o_ref[:, cut] = (mixed[n, ones_rows:, :] / mixed[n, 0:1, :]).astype(jnp.bfloat16)
 
 
 def attend(q_all, kv_all, pad_lengths):
     blocks, span, lanes = kv_all.shape
     total = q_all.shape[1]
     width = math.gcd(total, 4096)
+    group = math.gcd(width, 256)
+    groups = width // group
     return pl.pallas_call(
         attend_kernel,
         out_shape=jax.ShapeDtypeStruct((HD, total), jnp.bfloat16),
@@ -793,6 +816,10 @@
                 pltpu.VMEM(((blocks + 1) * span, lanes), jnp.bfloat16),
                 pltpu.VMEM((blocks + 1, HD + 16, span), jnp.bfloat16),
                 pltpu.SMEM((1,), jnp.int32),
+                pltpu.VMEM((groups, span, group), jnp.float32),
+                pltpu.VMEM((groups, 1, group), jnp.float32),
+                pltpu.VMEM((groups, 1, group), jnp.float32),
+                pltpu.VMEM((groups, HD + 16, group), jnp.float32),
             ],
         ),
         compiler_params=pltpu.CompilerParams(

time: 153 us -> 145 us (0.948); the launches traced: 151 us -> 145 us
  Pallas kernels: 148 us -> 142 us
    pallas_call x1, Pallas kernels: 26.7 us -> 21.4 us  [attend(): pl.pallas_call(attend_kernel, out_shape=jax.ShapeDtypeStruct((HD, total),...]
where the time goes in v5:
time: 145 us
  Pallas kernels  142 us (98%)
  local copies, waits for them, and re-layouts  2.06 us (1%)
    pallas_call x1, Pallas kernels, encoder_block(): pl.pallas_call(functools.partial(block_kernel, ring, share, sides), out_s...  79.2 us
    pallas_call x1, Pallas kernels, scatter_heads(): pl.pallas_call(functools.partial(scatter_kernel, ring, share, sides), out...  41.8 us
    pallas_call x1, Pallas kernels, attend(): pl.pallas_call(attend_kernel, out_shape=jax.ShapeDtypeStruct((HD, total),...  21.4 us

profile of v5, /device:TPU:0, one launch (start us, length us, event | category | flops | bytes accessed | tf_op | source)
XLA Modules:
  0.0 145.2 jit_solution(12131906048303958259)
XLA Ops:
  0.6 0.0 copy-start.4
  0.6 41.8 %scatter_heads.1 = (bf16[16,64,256]{2,1,0:T(8,128)(2,1)S(1)}, bf16[16,512,128]{2,1,0:T(8,128)(2,1)S(1)}, bf16[2,512,1024]{2,1,0:T(8,128)(2,1)S(1)}, bf16[256,512]{1,0:T(8,128)(2,1)S(1)}) custom-call(bf16[512,1024]{1,0:T(8,128)(2,1)} %tokens_hbm.3, f32[1,1024]{1,0:T(1,128)} %bitcast.20, bf16[3,1024,512]{2,1,0:T(8,128)(2,1)} %qkv_hbm.1, ...), custom_call_target="tpu_custom_call" | custom-call | tf_op jit(solution)/shard_map/scatter_heads/pallas_call | solution.py:236
  42.4 0.0 copy-start.1
  42.5 0.0 copy-start
  42.5 0.0 copy-start.2
  42.5 0.0 copy-start.3
  42.5 0.0 copy-start.5
  42.5 0.0 copy-done.4
  42.6 21.4 %attend.1 = bf16[64,4096]{1,0:T(8,128)(2,1)S(1)} custom-call(s32[16]{0:T(128)S(1)} %copy-done.4, bf16[64,4096]{1,0:T(8,128)(2,1)S(1)} %bitcast.15, bf16[16,512,128]{2,1,0:T(8,128)(2,1)S(1)} %get-tuple-element.7.kv_ref), custom_call_target="tpu_custom_call" | custom-call | tf_op jit(solution)/shard_map/attend/pallas_call | solution.py:803
  64.0 0.0 copy-done.1
  64.0 0.0 copy-done
  64.0 0.0 copy-done.2
  64.1 0.0 copy-done.3
  64.1 0.0 copy-done.5
  64.1 79.2 %encoder_block.1 = (bf16[512,1024]{1,0:T(8,128)(2,1)S(1)}, bf16[512,1024]{1,0:T(8,128)(2,1)S(1)}) custom-call(bf16[16,64,256]{2,1,0:T(8,128)(2,1)S(1)} %bitcast.14, s32[16]{0:T(128)S(1)} %copy-done.4, s32[4]{0:T(128)S(1)} %copy-done.5, bf16[512,1024]{1,0:T(8,128)(2,1)S(1)} %copy-done, f32[1,1024]{1,0:T(1,128)S(1)} %bitcast.18, f32[1,1024]{1,0:T(1,128)S(1)} %bitcast.19, ...), custom_call_target="tpu_custom_call" | custom-call | tf_op jit(solution)/shard_map/encoder_block/pallas_call | solution.py:666
  143.2 1.0 copy.26
  144.2 1.0 copy.27
  (2 shorter events, 0.1 us)
Async XLA Ops:
  0.6 41.9 %copy-start.4 = (s32[16]{0:T(128)S(1)}, s32[16]{0:T(128)}, u32[]{:S(2)}) copy-start(s32[16]{0:T(128)} %pad_lengths.1) | copy-start | bytes 196
  42.4 21.6 %copy-start.1 = (bf16[2,512,1024]{2,1,0:T(8,128)(2,1)}, bf16[2,512,1024]{2,1,0:T(8,128)(2,1)S(1)}, u32[]{:S(2)}) copy-start(bf16[2,512,1024]{2,1,0:T(8,128)(2,1)S(1)} %get-tuple-element.8.w_all_hbm) | copy-start | bytes 6291460
  42.5 21.6 %copy-start = (bf16[512,1024]{1,0:T(8,128)(2,1)S(1)}, bf16[512,1024]{1,0:T(8,128)(2,1)}, u32[]{:S(2)}) copy-start(bf16[512,1024]{1,0:T(8,128)(2,1)} %tokens_hbm.3) | copy-start | bytes 3145732
  42.5 21.6 %copy-start.2 = (f32[1024]{0:T(1024)S(1)}, f32[1024]{0:T(1024)}, u32[]{:S(2)}) copy-start(f32[1024]{0:T(1024)} %param.19) | copy-start | bytes 12292
  42.5 21.6 %copy-start.3 = (f32[1024]{0:T(1024)S(1)}, f32[1024]{0:T(1024)}, u32[]{:S(2)}) copy-start(f32[1024]{0:T(1024)} %param.22) | copy-start | bytes 12292
  42.5 21.6 %copy-start.5 = (s32[4]{0:T(128)S(1)}, s32[4]{0:T(128)}, u32[]{:S(2)}) copy-start(s32[4]{0:T(128)} %target_lengths.1) | copy-start | bytes 52

commit v6 on v5

--- a/solution.py
+++ b/solution.py
@@ -364,22 +364,25 @@
         load.wait()
     part = rows // share
 
-    def project(c, carry):
-        at = rows_at(c * part, part, part)
-        flat = context[c].reshape(sides * heads * HD, part)
+    chunk = math.gcd(rows, 128)
+    chunks = rows // chunk
+    unit = math.gcd(part, chunk)
+
+    def project(u):
+        at = rows_at(u * unit, unit, unit)
+        block = context.at[lax.div(u * unit, part)]
+        if unit < part:
+            block = block.at[:, :, rows_at(lax.rem(u * unit, part), unit, unit)]
         total = tokens[at, :].astype(jnp.float32) + lax.dot_general(
-            flat, w_out[...].reshape(sides * heads * HD, width), (((0,), (0,)), ((), ())),
+            block[...].reshape(sides * heads * HD, unit),
+            w_out[...].reshape(sides * heads * HD, width), (((0,), (0,)), ((), ())),
             preferred_element_type=jnp.float32,
         )
         hidden[at, :] = total
         normed[at, :] = norm_rows(total, g_ffn[...]).astype(jnp.bfloat16)
-        return carry
-
-    lax.fori_loop(0, share, project, 0)
+
     for load in loads[3:6]:
         load.wait()
-    chunk = math.gcd(rows, 128)
-    chunks = rows // chunk
 
     def span(c):
         return rows_at(c * chunk, chunk, chunk)
@@ -390,6 +393,8 @@
         )
 
     def feed(c, carry):
+        for n in range(chunk // unit):
+            project(c * (chunk // unit) + n)
         x = normed[span(c), :]
         gate = jnp.dot(x, up[0], preferred_element_type=jnp.float32)
         lift = jnp.dot(x, up[1], preferred_element_type=jnp.float32)

time: 145 us -> 144 us (level)
  no operation moved by 1% of the time
where the time goes in v6:
time: 144 us
  Pallas kernels  141 us (98%)
  local copies, waits for them, and re-layouts  2.06 us (1%)
    pallas_call x1, Pallas kernels, encoder_block(): pl.pallas_call(functools.partial(block_kernel, ring, share, sides), out_s...  77.9 us
    pallas_call x1, Pallas kernels, scatter_heads(): pl.pallas_call(functools.partial(scatter_kernel, ring, share, sides), out...  41.8 us
    pallas_call x1, Pallas kernels, attend(): pl.pallas_call(attend_kernel, out_shape=jax.ShapeDtypeStruct((HD, total),...  21.4 us

profile of v6, /device:TPU:0, one launch (start us, length us, event | category | flops | bytes accessed | tf_op | source)
XLA Modules:
  0.0 144.0 jit_solution(1815735334139399326)
XLA Ops:
  0.6 0.0 copy-start.4
  0.6 41.8 %scatter_heads.1 = (bf16[16,64,256]{2,1,0:T(8,128)(2,1)S(1)}, bf16[16,512,128]{2,1,0:T(8,128)(2,1)S(1)}, bf16[2,512,1024]{2,1,0:T(8,128)(2,1)S(1)}, bf16[256,512]{1,0:T(8,128)(2,1)S(1)}) custom-call(bf16[512,1024]{1,0:T(8,128)(2,1)} %tokens_hbm.3, f32[1,1024]{1,0:T(1,128)} %bitcast.20, bf16[3,1024,512]{2,1,0:T(8,128)(2,1)} %qkv_hbm.1, ...), custom_call_target="tpu_custom_call" | custom-call | tf_op jit(solution)/shard_map/scatter_heads/pallas_call | solution.py:236
  42.4 0.0 copy-start.1
  42.5 0.0 copy-start
  42.5 0.0 copy-start.2
  42.5 0.0 copy-start.3
  42.5 0.0 copy-start.5
  42.5 0.0 copy-done.4
  42.6 21.4 %attend.1 = bf16[64,4096]{1,0:T(8,128)(2,1)S(1)} custom-call(s32[16]{0:T(128)S(1)} %copy-done.4, bf16[64,4096]{1,0:T(8,128)(2,1)S(1)} %bitcast.15, bf16[16,512,128]{2,1,0:T(8,128)(2,1)S(1)} %get-tuple-element.7.kv_ref), custom_call_target="tpu_custom_call" | custom-call | tf_op jit(solution)/shard_map/attend/pallas_call | solution.py:808
  64.0 0.0 copy-done.1
  64.0 0.0 copy-done
  64.0 0.0 copy-done.2
  64.1 0.0 copy-done.3
  64.1 0.0 copy-done.5
  64.1 77.9 %encoder_block.1 = (bf16[512,1024]{1,0:T(8,128)(2,1)S(1)}, bf16[512,1024]{1,0:T(8,128)(2,1)S(1)}) custom-call(bf16[16,64,256]{2,1,0:T(8,128)(2,1)S(1)} %bitcast.14, s32[16]{0:T(128)S(1)} %copy-done.4, s32[4]{0:T(128)S(1)} %copy-done.5, bf16[512,1024]{1,0:T(8,128)(2,1)S(1)} %copy-done, f32[1,1024]{1,0:T(1,128)S(1)} %bitcast.18, f32[1,1024]{1,0:T(1,128)S(1)} %bitcast.19, ...), custom_call_target="tpu_custom_call" | custom-call | tf_op jit(solution)/shard_map/encoder_block/pallas_call | solution.py:671
  142.0 1.0 copy.26
  143.0 1.0 copy.27
  (2 shorter events, 0.1 us)
Async XLA Ops:
  0.6 41.9 %copy-start.4 = (s32[16]{0:T(128)S(1)}, s32[16]{0:T(128)}, u32[]{:S(2)}) copy-start(s32[16]{0:T(128)} %pad_lengths.1) | copy-start | bytes 196
  42.4 21.6 %copy-start.1 = (bf16[2,512,1024]{2,1,0:T(8,128)(2,1)}, bf16[2,512,1024]{2,1,0:T(8,128)(2,1)S(1)}, u32[]{:S(2)}) copy-start(bf16[2,512,1024]{2,1,0:T(8,128)(2,1)S(1)} %get-tuple-element.8.w_all_hbm) | copy-start | bytes 6291460
  42.5 21.6 %copy-start = (bf16[512,1024]{1,0:T(8,128)(2,1)S(1)}, bf16[512,1024]{1,0:T(8,128)(2,1)}, u32[]{:S(2)}) copy-start(bf16[512,1024]{1,0:T(8,128)(2,1)} %tokens_hbm.3) | copy-start | bytes 3145732
  42.5 21.6 %copy-start.2 = (f32[1024]{0:T(1024)S(1)}, f32[1024]{0:T(1024)}, u32[]{:S(2)}) copy-start(f32[1024]{0:T(1024)} %param.19) | copy-start | bytes 12292
  42.5 21.6 %copy-start.3 = (f32[1024]{0:T(1024)S(1)}, f32[1024]{0:T(1024)}, u32[]{:S(2)}) copy-start(f32[1024]{0:T(1024)} %param.22) | copy-start | bytes 12292
  42.5 21.6 %copy-start.5 = (s32[4]{0:T(128)S(1)}, s32[4]{0:T(128)}, u32[]{:S(2)}) copy-start(s32[4]{0:T(128)} %target_lengths.1) | copy-start | bytes 52
